TPU v7x, 128 devices: a whole 4x4x4 slice. The times are simulated.
128 devices in a mesh: dp: 4 (over y), col: 32 (over z, x, core).
Axes of the slice: x: 4, y: 4, z: 4, core: 2. Of those that a mesh axis runs over, the one named last changes fastest.
Arguments:
- tokens: bfloat16 [1536, 2304], P('dp', 'col'), may hold values from -6 to 6
- cotangent: bfloat16 [1536, 2304], P('dp', 'col'), may hold values from -6 to 6
- prefix: int32 [12], P('dp'), may hold values from 0 to 3
- gate_weight: bfloat16 [2304, 36864], P(None, 'col'), may hold values from -0.125 to 0.125
- up_weight: bfloat16 [2304, 36864], P(None, 'col'), may hold values from -0.125 to 0.125
- down_weight: bfloat16 [36864, 2304], P('col'), may hold values from -0.0625 to 0.0625
Outputs:
- output: bfloat16 [1536, 2304], P('dp', 'col')
- input_grad: bfloat16 [1536, 2304], P('dp', 'col')
- grad_gate: bfloat16 [2304, 36864], P('dp', 'col')
- grad_up: bfloat16 [2304, 36864], P('dp', 'col')
- grad_down: bfloat16 [36864, 2304], P('col', 'dp')
All inputs are finite; a program needn't handle non-finite values.
Results may differ from a plain program's by a relative error of at most 0.017.
Values may be sent and summed in bfloat16 or wider, within the bound.
A program may use at most 128 MiB of HBM per device.

v0:
```python
import jax
import jax.numpy as jnp
from jax import lax
from jax.sharding import PartitionSpec as P

FF = 36864
BLOCK = 128


def rows_first(arrays, axis, dims):
    turned = [jnp.moveaxis(a, dim, 0) for a, dim in zip(arrays, dims)]
    widths = [t[0].size for t in turned]
    both = jnp.concatenate([t.reshape(-1, w) for t, w in zip(turned, widths)], axis=1)
    whole = lax.all_gather(both, axis, axis=0, tiled=True)
    blocks = jnp.split(whole, [sum(widths[:k]) for k in range(1, len(widths))], axis=1)
    return tuple(
        (
            jnp.moveaxis(b.reshape(-1, *t.shape[1:]), 0, dim)
            for b, t, dim in zip(blocks, turned, dims)
        )
    )


def split_up(value, dim, count):
    shape = value.shape
    blocks = value.reshape(*shape[:dim], count, shape[dim] // count, *shape[dim + 1 :])
    return jnp.moveaxis(blocks, dim, 0)


def summed_on_arrival(value, axis, dim):
    blocks = split_up(value, dim, lax.axis_size(axis))
    arrived = lax.all_to_all(blocks, axis, split_axis=0, concat_axis=0, tiled=True)
    return arrived.astype(jnp.float32).sum(axis=0)


def joined_along(blocks, dim):
    blocks = jnp.moveaxis(blocks, 0, dim)
    shape = blocks.shape
    return blocks.reshape(*shape[:dim], shape[dim] * shape[dim + 1], *shape[dim + 2 :])


def one_gather(arrays, axis, dims):
    ravelled = jnp.concatenate([a.reshape(-1) for a in arrays])
    lines, at, finished = (lax.all_gather(ravelled, axis), 0, [])
    for a, dim in zip(arrays, dims):
        blocks = lines[:, at : at + a.size].reshape(-1, *a.shape)
        finished.append(joined_along(blocks, dim))
        at += a.size
    return tuple(finished)


def gelu_pair(value):
    scale = 0.7978845608028654
    inner = jnp.tanh(scale * (value + 0.044715 * value * value * value))
    act = 0.5 * value * (1.0 + inner)
    slope = 0.5 * (1.0 + inner) + 0.5 * value * (1.0 - inner * inner) * scale * (
        1.0 + 3.0 * 0.044715 * value * value
    )
    return (act, slope)


def contract_last(left, right):
    return lax.dot_general(
        left, right, (((1,), (1,)), ((), ())), preferred_element_type=jnp.float32
    )


def body(tokens, cotangent, prefix, gate_weight, up_weight, down_weight):
    whole, grad_out = rows_first((tokens, cotangent), "col", (1, 1))
    rows = whole.shape[0]
    local = gate_weight.shape[1]
    start = lax.axis_index("col") * local
    columns = start + jnp.arange(local, dtype=jnp.int32)
    widths = jnp.left_shift(jnp.int32(FF // 8), prefix)
    per_token = jnp.repeat(widths, BLOCK, total_repeat_length=rows)
    mask = (columns[None, :] < per_token[:, None]).astype(jnp.float32)
    gate = jnp.dot(whole, gate_weight, preferred_element_type=jnp.float32)
    up = jnp.dot(whole, up_weight, preferred_element_type=jnp.float32)
    act, slope = gelu_pair(gate)
    hidden = (mask * act * up).astype(jnp.bfloat16)
    partial_value = jnp.dot(hidden, down_weight, preferred_element_type=jnp.float32)
    back = contract_last(grad_out, down_weight)
    dgate = (mask * back * up * slope).astype(jnp.bfloat16)
    dup = (mask * back * act).astype(jnp.bfloat16)
    toward = contract_last(dgate, gate_weight) + contract_last(dup, up_weight)
    output = summed_on_arrival(partial_value.astype(jnp.bfloat16), "col", 1).astype(jnp.bfloat16)
    input_grad = summed_on_arrival(toward.astype(jnp.bfloat16), "col", 1).astype(jnp.bfloat16)
    both = jnp.concatenate([dgate, dup], axis=1)
    own_x, own_dy = (
        lax.all_to_all(whole, "dp", split_axis=1, concat_axis=0, tiled=True),
        lax.all_to_all(grad_out, "dp", split_axis=1, concat_axis=0, tiled=True),
    )
    all_both, all_hidden = one_gather((both, hidden), "dp", (0, 0))
    groups = lax.axis_size("dp")
    x_groups = own_x.reshape(groups, rows, -1)
    dy_groups = own_dy.reshape(groups, rows, -1)
    first = jnp.einsum(
        "gtd,gtf->gdf",
        x_groups,
        all_both.reshape(groups, rows, -1),
        preferred_element_type=jnp.float32,
    )
    second = jnp.einsum(
        "gtd,gtf->gdf",
        dy_groups,
        all_hidden.reshape(groups, rows, -1),
        preferred_element_type=jnp.float32,
    )
    stacked = jnp.concatenate([first, second], axis=2)
    summed = jnp.sum(stacked.astype(jnp.bfloat16).astype(jnp.float32), axis=0)
    grads = summed.astype(jnp.bfloat16).reshape(summed.shape[0], 3, local)
    return (output, input_grad, grads[:, 0], grads[:, 1], grads[:, 2].T)


def solution(mesh):
    return jax.shard_map(
        body,
        mesh=mesh,
        in_specs=(
            P("dp", "col"),
            P("dp", "col"),
            P("dp"),
            P(None, "col"),
            P(None, "col"),
            P("col", None),
        ),
        out_specs=(P("dp", "col"), P("dp", "col"), P("dp", "col"), P("dp", "col"), P("col", "dp")),
        check_vma=False,
    )
```

profile of v0, /device:TPU:0, one launch (start us, length us, event | category | flops | bytes accessed | tf_op | source)
XLA Modules:
  0.0 272.2 jit_solution(6095015435056827527)
XLA Ops:
  7.2 0.0 all-gather.4.cloned.1.call-start
  7.2 1.5 pad_maximum_fusion.2
  8.7 0.0 all-gather.4.cloned.1.call-update
  8.7 0.0 all-gather.6.cloned.1.call-start
  8.8 0.7 broadcast_shift-left_fusion
  9.5 0.6 fusion.27
  10.1 2.0 fusion.20
  12.0 46.8 %all-gather.4.cloned.1.call-done = bf16[2304,768]{1,0:T(8,128)(2,1)} async-done(((bf16[72,768]{1,0:T(8,128)(2,1)}), bf16[2304,768]{1,0:T(8,128)(2,1)}) %all-gather.4.cloned.1.call-update) | async-done | bytes 3538960 | tf_op jit(solution)/shard_map/all_gather | solution.py:14
  58.8 0.0 slice-start.1
  58.8 5.7 %fusion.24 = f32[384,1152]{1,0:T(8,128)S(1)} fusion(bf16[2304,1152]{1,0:T(8,128)(2,1)} %param.11, bf16[2304,768]{1,0:T(8,128)(2,1)} %all-gather.4.cloned.1.call-done), kind=kOutput, calls=%fused_computation.49 | convolution fusion | flops 2038431744 | bytes 8847360 | tf_op jit(solution)/shard_map/dot_general | solution.py:77
  64.5 0.0 copy-done.1
  64.5 0.0 slice-start.2
  64.5 5.2 %fusion.22 = f32[384,1152]{1,0:T(8,128)S(1)} fusion(bf16[2304,1152]{1,0:T(8,128)(2,1)} %param.12, bf16[2304,768]{1,0:T(8,128)(2,1)S(1)} %copy-done.1), kind=kOutput, calls=%fused_computation.47 | convolution fusion | flops 2038431744 | bytes 8847360 | tf_op jit(solution)/shard_map/dot_general | solution.py:78
  69.7 0.0 slice-done.1
  69.7 0.0 slice-done.2
  69.7 3.9 %multiply_convert_fusion = (bf16[384,1152]{1,0:T(8,128)(2,1)S(1)}, bf16[384,1152]{1,0:T(8,128)(2,1)S(1)}, bf16[384,1152]{1,0:T(8,128)(2,1)S(1)}) fusion(f32[384,1152]{1,0:T(8,128)S(1)} %fusion.24, f32[384,1152]{1,0:T(8,128)S(1)} %fusion.22, s32[384]{0:T(512)S(1)} %and_select_fusion, s32[1152]{0:T(1024)S(1)} %iota_add_fusion, ...), kind=kOutput, calls=%fused_computation.27 | convolution fusion | flops 2050818048 | bytes 13281280 | tf_op jit(solution)/shard_map/dot_general | solution.py:63
  73.7 0.0 copy-start.8
  73.7 0.0 copy-start.4
  73.7 0.0 copy-start.6
  73.7 1.8 reshape.132
  75.6 0.0 copy-done.8
  75.6 0.0 copy-done.4
  75.6 0.0 copy-done.6
  75.6 0.1 pad_maximum_fusion.1
  75.7 2.0 reshape.131
  77.7 5.2 %pad_maximum_fusion = bf16[1327104]{0:T(1024)(128)(2,1)} fusion(bf16[442368]{0:T(1024)(128)(2,1)} %reshape.132, bf16[884736]{0:T(1024)(128)(2,1)S(1)} %reshape.131), kind=kLoop, calls=%fused_computation.11 | loop fusion | flops 5308416 | bytes 5308416 | tf_op jit(solution)/shard_map/concatenate | solution.py:43
  82.9 0.0 all-gather.6.cloned.1.call-update
  82.9 4.1 %fusion.26 = (bf16[2304,384]{1,0:T(8,128)(2,1)}, bf16[2304,384]{1,0:T(8,128)(2,1)}) fusion(bf16[2304,768]{1,0:T(8,128)(2,1)} %all-gather.4.cloned.1.call-done), kind=kLoop, calls=%fused_computation.51 | loop fusion | bytes 7077888 | tf_op jit(solution)/shard_map/split | solution.py:15
  87.1 4.3 %all-to-all-start.3 = ((bf16[384,4,576]{0,2,1:T(8,128)(2,1)}), bf16[384,4,576]{0,2,1:T(8,128)(2,1)S(1)}, u32[]{:S(2)}, u32[]{:S(2)}) async-start(bf16[384,4,576]{0,2,1:T(8,128)(2,1)} %bitcast.15), calls=%async_computation.3 | async-start | bytes 3538944 | tf_op jit(solution)/shard_map/all_to_all | solution.py:91
  91.4 6.2 %convolution_convert_fusion.2 = bf16[384,2304]{1,0:T(8,128)(2,1)S(1)} fusion(bf16[384,1152]{1,0:T(8,128)(2,1)} %copy-done.8, bf16[1152,2304]{1,0:T(8,128)(2,1)} %param.13), kind=kOutput, calls=%fused_computation.7 | convolution fusion | flops 2039316480 | bytes 7962624 | tf_op jit(solution)/shard_map/dot_general | solution.py:81
  97.6 2.2 copy.16
  99.8 31.7 %all-to-all-done.3 = bf16[384,4,576]{0,2,1:T(8,128)(2,1)S(1)} async-done(((bf16[384,4,576]{0,2,1:T(8,128)(2,1)}), bf16[384,4,576]{0,2,1:T(8,128)(2,1)S(1)}, u32[]{:S(2)}, u32[]{:S(2)}) %all-to-all-start.3) | async-done | bytes 1769504 | tf_op jit(solution)/shard_map/all_to_all | solution.py:91
  131.5 0.0 copy-start.2
  131.5 0.0 copy-start.7
  131.5 1.2 copy-done.2
  132.8 4.0 %all-to-all-start = ((bf16[32,384,72]{1,2,0:T(8,128)(2,1)}), bf16[32,384,72]{1,2,0:T(8,128)(2,1)S(1)}, u32[]{:S(2)}, u32[]{:S(2)}) async-start(bf16[32,384,72]{1,2,0:T(8,128)(2,1)} %bitcast.8), calls=%async_computation | async-start | bytes 3538944 | tf_op jit(solution)/shard_map/all_to_all | solution.py:32
  136.8 0.0 copy-done.7
  136.8 0.0 copy-start.5
  136.8 5.2 %fusion.28 = f32[384,2304]{1,0:T(8,128)S(1)} fusion(bf16[384,1152]{1,0:T(8,128)(2,1)S(1)} %copy-done.7, bf16[2304,1152]{1,0:T(8,128)(2,1)} %param.11), kind=kOutput, calls=%fused_computation.53 | convolution fusion | flops 2038431744 | bytes 9732096 | tf_op jit(solution)/shard_map/dot_general | solution.py:63
  142.0 0.0 copy-done.5
  142.0 5.1 %fusion.2 = bf16[384,2304]{1,0:T(8,128)(2,1)S(1)} fusion(f32[384,2304]{1,0:T(8,128)S(1)} %fusion.28, bf16[384,1152]{1,0:T(8,128)(2,1)S(1)} %copy-done.5, bf16[2304,1152]{1,0:T(8,128)(2,1)} %param.12), kind=kOutput, calls=%fused_computation.6 | convolution fusion | flops 2040201216 | bytes 11501568 | tf_op jit(solution)/shard_map/dot_general | solution.py:63
  147.1 2.2 copy.17
  149.3 13.8 %all-to-all-done = bf16[32,384,72]{1,2,0:T(8,128)(2,1)S(1)} async-done(((bf16[32,384,72]{1,2,0:T(8,128)(2,1)}), bf16[32,384,72]{1,2,0:T(8,128)(2,1)S(1)}, u32[]{:S(2)}, u32[]{:S(2)}) %all-to-all-start) | async-done | bytes 1769504 | tf_op jit(solution)/shard_map/all_to_all | solution.py:32
  163.1 29.0 %all_to_all.42 = bf16[32,384,72]{1,2,0:T(8,128)(2,1)S(1)} all-to-all(bf16[32,384,72]{1,2,0:T(8,128)(2,1)} %bitcast.72), channel_id=1, replica_groups=mesh['dp'=4,'col'=32] {'col'}, dimensions={0} | all-to-all | bytes 3538944 | tf_op jit(solution)/shard_map/all_to_all | solution.py:32
  192.1 4.6 %all-to-all-start.2 = ((bf16[384,4,576]{0,2,1:T(8,128)(2,1)}), bf16[384,4,576]{0,2,1:T(8,128)(2,1)}, u32[]{:S(2)}, u32[]{:S(2)}) async-start(bf16[384,4,576]{0,2,1:T(8,128)(2,1)} %bitcast.12), calls=%async_computation.2 | async-start | bytes 3538944 | tf_op jit(solution)/shard_map/all_to_all | solution.py:90
  196.7 0.9 reduce_sum.36
  197.6 0.9 reduce_sum.37
  198.5 1.5 all-gather.6.cloned.1.call-done
  200.0 13.6 %reshape.144 = bf16[4,1327104]{1,0:T(4,128)(2,1)} reshape(bf16[5308416]{0:T(1024)(128)(2,1)} %all-gather.6.cloned.1.call-done) | data formatting | bytes 21233664 | tf_op jit(solution)/shard_map/all_gather | solution.py:44
  213.6 0.0 slice-start
  213.6 0.0 copy-start.3
  213.6 8.6 %slice.40 = bf16[4,884736]{1,0:T(4,128)(2,1)} slice(bf16[4,1327104]{1,0:T(4,128)(2,1)} %reshape.144), slice={[0:4], [0:884736]} | slice | bytes 14155776 | tf_op jit(solution)/shard_map/slice | solution.py:46
  222.2 0.0 slice-done
  222.2 0.0 copy-done.3
  222.2 5.0 %convolution_convert_fusion.1 = bf16[4,576,1152]{2,1,0:T(8,128)(2,1)} fusion(bf16[1,4,384,1152]{3,1,2,0:T(4,128)(2,1)S(1)} %bitcast.69, bf16[384,4,576]{0,2,1:T(8,128)(2,1)S(1)} %copy-done.3), kind=kOutput, calls=%fused_computation.4 | convolution fusion | flops 2041085952 | bytes 10616832 | tf_op jit(solution)/shard_map/gtd,gtf->gdf/dot_general | solution.py:103
  227.2 0.0 all-to-all-done.2
  227.2 11.6 %convolution_convert_fusion = bf16[4,576,2304]{2,1,0:T(8,128)(2,1)} fusion(bf16[1,4,384,2304]{3,1,2,0:T(4,128)(2,1)} %bitcast.71, bf16[384,4,576]{0,2,1:T(8,128)(2,1)} %all-to-all-done.2), kind=kOutput, calls=%fused_computation.1 | convolution fusion | flops 4082171904 | bytes 19464192 | tf_op jit(solution)/shard_map/gtd,gtf->gdf/dot_general | solution.py:97
  238.8 0.0 copy-done
  238.8 10.2 %maximum_reduce_fusion = bf16[576,3456]{1,0:T(8,128)(2,1)} fusion(bf16[4,576,1152]{2,1,0:T(8,128)(2,1)S(1)} %copy-done, bf16[4,576,2304]{2,1,0:T(8,128)(2,1)} %convolution_convert_fusion), kind=kLoop, calls=%fused_computation | loop fusion | flops 37822464 | bytes 19906560 | tf_op jit(solution)/shard_map/reduce_sum | solution.py:110
  249.0 6.4 %copy.18 = bf16[576,3456]{0,1:T(8,128)(2,1)} copy(bf16[576,3456]{1,0:T(8,128)(2,1)} %maximum_reduce_fusion) | data formatting | bytes 7962624 | tf_op jit(solution)/shard_map/reduce_sum | solution.py:110
  255.5 3.8 %slice_bitcast_fusion = (bf16[1152,576]{1,0:T(8,128)(2,1)S(1)}, bf16[576,1152]{0,1:T(8,128)(2,1)S(1)}, bf16[576,1152]{0,1:T(8,128)(2,1)}) fusion(bf16[576,3,1152]{0,2,1:T(8,128)(2,1)} %bitcast.70), kind=kLoop, calls=%fused_computation.29 | loop fusion | bytes 7962624 | tf_op jit(solution)/shard_map/transpose | solution.py:112
  259.3 2.6 copy.19
  261.8 1.7 copy.20
  263.6 1.7 copy.21
  (6 shorter events, 0.0 us)
Async XLA Ops:
  7.2 51.6 %all-gather.4.cloned.1.call-start = ((), (), s32[]{:S(2)}) async-start(), calls=%async_computation.4 | async-start | bytes 3649536 | tf_op jit(solution)/shard_map/all_gather | solution.py:14
  8.7 191.2 %all-gather.6.cloned.1.call-start = ((), (), s32[]{:S(2)}) async-start(), calls=%async_computation.5 | async-start | bytes 13271040 | tf_op jit(solution)/shard_map/all_gather | solution.py:44
  58.8 5.7 %copy-start.1 = (bf16[2304,768]{1,0:T(8,128)(2,1)S(1)}, bf16[2304,768]{1,0:T(8,128)(2,1)}, u32[]{:S(2)}) copy-start(bf16[2304,768]{1,0:T(8,128)(2,1)} %all-gather.4.cloned.1.call-done) | copy-start | bytes 10616836
  58.8 10.9 %slice-start.1 = ((s8[5308416]{0:T(1024)(128)(4,1)}), s8[4194304]{0:T(1024)(128)(4,1)S(1)}, s32[]{:S(2)}) async-start(s8[5308416]{0:T(1024)(128)(4,1)} %bitcast.75), calls=%async_computation.7 | async-start | bytes 8388608
  64.5 5.2 %slice-start.2 = ((s8[5308416]{0:T(1024)(128)(4,1)}), s8[1114112]{0:T(1024)(128)(4,1)S(1)}, s32[]{:S(2)}) async-start(s8[5308416]{0:T(1024)(128)(4,1)} %bitcast.75), calls=%async_computation.8 | async-start | bytes 2228224
  73.7 1.9 copy-start.8
  73.7 1.9 copy-start.4
  73.7 1.9 copy-start.6
  87.1 44.5 %all-to-all-start.3 = ((bf16[384,4,576]{0,2,1:T(8,128)(2,1)}), bf16[384,4,576]{0,2,1:T(8,128)(2,1)S(1)}, u32[]{:S(2)}, u32[]{:S(2)}) async-start(bf16[384,4,576]{0,2,1:T(8,128)(2,1)} %bitcast.15), calls=%async_computation.3 | async-start | bytes 3538944 | tf_op jit(solution)/shard_map/all_to_all | solution.py:91
  131.5 1.2 copy-start.2
  131.5 5.2 %copy-start.7 = (bf16[384,1152]{1,0:T(8,128)(2,1)S(1)}, bf16[384,1152]{1,0:T(8,128)(2,1)}, u32[]{:S(2)}) copy-start(bf16[384,1152]{1,0:T(8,128)(2,1)} %copy-done.6) | copy-start | bytes 2654212
  132.8 30.3 %all-to-all-start = ((bf16[32,384,72]{1,2,0:T(8,128)(2,1)}), bf16[32,384,72]{1,2,0:T(8,128)(2,1)S(1)}, u32[]{:S(2)}, u32[]{:S(2)}) async-start(bf16[32,384,72]{1,2,0:T(8,128)(2,1)} %bitcast.8), calls=%async_computation | async-start | bytes 3538944 | tf_op jit(solution)/shard_map/all_to_all | solution.py:32
  136.8 5.2 %copy-start.5 = (bf16[384,1152]{1,0:T(8,128)(2,1)S(1)}, bf16[384,1152]{1,0:T(8,128)(2,1)}, u32[]{:S(2)}) copy-start(bf16[384,1152]{1,0:T(8,128)(2,1)} %copy-done.4) | copy-start | bytes 2654212
  192.1 35.0 %all-to-all-start.2 = ((bf16[384,4,576]{0,2,1:T(8,128)(2,1)}), bf16[384,4,576]{0,2,1:T(8,128)(2,1)}, u32[]{:S(2)}, u32[]{:S(2)}) async-start(bf16[384,4,576]{0,2,1:T(8,128)(2,1)} %bitcast.12), calls=%async_computation.2 | async-start | bytes 3538944 | tf_op jit(solution)/shard_map/all_to_all | solution.py:90
  213.6 8.6 %slice-start = ((bf16[4,1327104]{1,0:T(4,128)(2,1)}), bf16[4,442368]{1,0:T(4,128)(2,1)S(1)}, s32[]{:S(2)}) async-start(bf16[4,1327104]{1,0:T(4,128)(2,1)} %reshape.144), calls=%async_computation.6 | async-start | bytes 7077888 | tf_op jit(solution)/shard_map/slice | solution.py:46
  213.6 8.6 %copy-start.3 = (bf16[384,4,576]{0,2,1:T(8,128)(2,1)S(1)}, bf16[384,4,576]{0,2,1:T(8,128)(2,1)}, u32[]{:S(2)}) copy-start(bf16[384,4,576]{0,2,1:T(8,128)(2,1)} %copy-done.2) | copy-start | bytes 5308420
  227.2 11.6 %copy-start = (bf16[4,576,1152]{2,1,0:T(8,128)(2,1)S(1)}, bf16[4,576,1152]{2,1,0:T(8,128)(2,1)}, u32[]{:S(2)}) copy-start(bf16[4,576,1152]{2,1,0:T(8,128)(2,1)} %convolution_convert_fusion.1) | copy-start | bytes 15925252
Sparse Core Ops, SparseCore 0:
  10.9 47.8 all-gather.3
  83.1 116.8 all-gather.5
where the time goes:
time: 274 us; the launch traced here: 272 us
  waiting for transfers between devices  93.8 us (34%)
  local copies, waits for them, and re-layouts  52.9 us (19%)
  matrix products  47.9 us (17%)
  blocking collectives  29 us (11%)
  other arithmetic  21.4 us (8%)
  between operations  14.2 us (5%)
  starting transfers between devices  13 us (5%)
    all_gather x1, waiting for transfers between devices, rows_first(): whole = lax.all_gather(both, axis, axis=0, tiled=True)  46.8 us
    all_to_all x1, waiting for transfers between devices, body(): lax.all_to_all(grad_out, 'dp', split_axis=1, concat_axis=0, tiled=True)  31.7 us
    all_to_all x1, blocking collectives, summed_on_arrival(): lax.all_to_all(blocks, axis, split_axis=0, concat_axis=0, tiled=True)  29 us
    dot_general x3, matrix products, contract_last(): lax.dot_general(left, right, (((1,), (1,)), ((), ())), preferred_element_...  14.2 us
    all_to_all x1, waiting for transfers between devices, summed_on_arrival(): lax.all_to_all(blocks, axis, split_axis=0, concat_axis=0, tiled=True)  13.8 us
    all_gather x1, local copies, waits for them, and re-layouts, one_gather(): lines, at, finished = (lax.all_gather(ravelled, axis), 0, [])  13.6 us
    dot_general x1, matrix products, body(): jnp.einsum('gtd,gtf->gdf', x_groups, all_both.reshape(groups, rows, -1),...  11.6 us
    reduce_sum x1, other arithmetic, body(): summed = jnp.sum(stacked.astype(jnp.bfloat16).astype(jnp.float32), axis=0)  10.2 us
  transfers between devices with their start and end apart: 5, of which 4 were waited for; matrix products, arithmetic and copies ran while one was open for 21% of the time, Pallas kernels for 0%

commit v1 on v0

v1 whole, which is shorter than its diff:
```python
import functools

import jax
import jax.numpy as jnp
from jax import lax
from jax.experimental import pallas as pl
from jax.experimental.pallas import tpu as pltpu
from jax.sharding import PartitionSpec as P

BF = jnp.bfloat16
F32 = jnp.float32
UNIT = 4608
BLOCK = 128
MESH = pl.DeviceIdType.MESH
TOP = 80


def contract(left, right, left_dim, right_dim):
    return lax.dot_general(
        left, right, (((left_dim,), (right_dim,)), ((), ())), preferred_element_type=F32
    )


def gelu_pair(value):
    scale = 0.7978845608028654
    square = value * value
    inner = jnp.tanh(value * (scale + (scale * 0.044715) * square))
    half = 0.5 + 0.5 * inner
    act = value * half
    slope = half + (0.5 * value) * (1.0 - inner * inner) * (
        scale + (3.0 * 0.044715 * scale) * square
    )
    return act, slope


def layer_kernel(
    z_in,
    prefix_in,
    gate_hbm,
    up_hbm,
    down_hbm,
    acts_hbm,
    own_hbm,
    result,
    gate_w,
    up_w,
    down_w,
    xx,
    z_sib,
    levels,
    gate_f,
    up_f,
    back_f,
    acts,
    part,
    part_sib,
    line_two,
    line_four,
    block_half,
    block_one,
    fin,
    fin_sib,
    w_sem,
    z_sem,
    lev_sem,
    y_sem,
    one_sem,
    two_sem,
    sib_sem,
    send_sem,
    sib_send_sem,
    misc_send,
    rs_sem,
    act_sem,
    own_sem,
):
    toks = z_in.shape[2]
    rows = 2 * z_in.shape[1]
    y = lax.axis_index("dp")
    c = lax.axis_index("col")
    h = lax.rem(c, 2)
    chip = c // 2
    zc = chip // 4
    xc = lax.rem(chip, 4)
    o = 1 - h

    def at(d1, d2):
        zz = lax.rem(zc + (d1 % 4) * h + (d2 % 4) * o, 4)
        xq = lax.rem(xc + (d1 % 4) * o + (d2 % 4) * h, 4)
        return zz * 4 + xq

    def dev(d1, d2):
        return (y, at(d1, d2) * 2 + h)

    def row(d1, d2):
        return pl.multiple_of(at(d1, d2) * rows, 16)

    one_p, one_m = dev(1, 0), dev(-1, 0)
    two_p, two_m = dev(0, 1), dev(0, -1)
    sib = (y, chip * 2 + o)
    y_p, y_m = (lax.rem(y + 1, 4), c), (lax.rem(y + 3, 4), c)

    def blk(s, d1, d2, lo=0, n=None):
        start = row(d1, d2)
        return xx.at[h, s, pl.ds(start + lo, rows if n is None else n), :]

    def rput(src, dst, ssem, rsem, to):
        pltpu.make_async_remote_copy(
            src_ref=src, dst_ref=dst, send_sem=ssem, recv_sem=rsem, device_id=to, device_id_type=MESH
        ).start()

    def await_(ref, sem):
        pltpu.make_async_copy(ref, ref, sem).wait()

    loads = [
        pltpu.make_async_copy(src, dst, w_sem.at[k])
        for k, (src, dst) in enumerate(((gate_hbm, gate_w), (up_hbm, up_w), (down_hbm, down_w)))
    ]
    for load in loads:
        load.start()

    barrier = pltpu.get_barrier_semaphore()
    for to in (sib, one_p, one_m, two_p, two_m, y_p, y_m):
        pl.semaphore_signal(barrier, inc=1, device_id=to, device_id_type=MESH)
    pl.semaphore_wait(barrier, 7)

    rput(z_in, z_sib, misc_send.at[0], z_sem.at[0], sib)
    levels[0] = prefix_in[...]
    await_(z_sib, z_sem.at[0])
    mine, other = z_in[h].astype(F32), z_sib[h].astype(F32)
    low = jnp.where(h == 0, mine, other)
    high = jnp.where(h == 0, other, mine)
    xx[h, 0, pl.ds(row(0, 0), rows), :] = jnp.concatenate([low, high], axis=0).astype(BF)

    rest = rows - TOP
    offs = (0, -1, 1, 2)

    def to_sib(s, d1, d2):
        rput(blk(s, d1, d2), blk(s, d1, d2), sib_send_sem.at[s], sib_sem.at[s], sib)

    def across(s, i):
        d1 = offs[i]
        b = blk(s, d1, 0)
        rput(b, b, send_sem.at[s], two_sem.at[s, i], two_p)
        rput(b, b, send_sem.at[s], two_sem.at[s, 4 + i], two_m)

    def ev_a(s):
        if s in (1, 2):
            await_(blk(s, 0, 0), y_sem.at[s - 1])
        if s == 3:
            await_(blk(s, 0, 0, 0, TOP), y_sem.at[2])
            await_(blk(s, 0, 0, TOP, rest), y_sem.at[3])
        b = blk(s, 0, 0)
        rput(b, b, send_sem.at[s], one_sem.at[s, 0], one_p)
        rput(b, b, send_sem.at[s], one_sem.at[s, 1], one_m)
        across(s, 0)
        to_sib(s, 0, 0)

    def ev_b(s):
        await_(blk(s, -1, 0), one_sem.at[s, 0])
        b = blk(s, -1, 0, 0, TOP)
        rput(b, b, send_sem.at[s], one_sem.at[s, 2], one_p)
        await_(blk(s, 1, 0), one_sem.at[s, 1])
        b = blk(s, 1, 0, TOP, rest)
        rput(b, b, send_sem.at[s], one_sem.at[s, 3], one_m)
        across(s, 1)
        across(s, 2)
        to_sib(s, -1, 0)
        to_sib(s, 1, 0)

    def from_two(s, i):
        d1 = offs[i]
        await_(blk(s, d1, -1), two_sem.at[s, i])
        if i in (0, 2):
            b = blk(s, d1, -1)
            rput(b, b, send_sem.at[s], two_sem.at[s, 8 + i], two_p)
        to_sib(s, d1, -1)
        await_(blk(s, d1, 1), two_sem.at[s, 4 + i])
        if i in (1, 3):
            b = blk(s, d1, 1)
            rput(b, b, send_sem.at[s], two_sem.at[s, 8 + i], two_m)
        to_sib(s, d1, 1)

    def ev_c(s):
        from_two(s, 0)
        await_(blk(s, 2, 0, 0, TOP), one_sem.at[s, 2])
        await_(blk(s, 2, 0, TOP, rest), one_sem.at[s, 3])
        across(s, 3)
        to_sib(s, 2, 0)

    def ev_d(s):
        from_two(s, 1)
        from_two(s, 2)
        from_two(s, 3)

    def ev_e(s):
        for i in range(4):
            await_(blk(s, offs[i], 2), two_sem.at[s, 8 + i])
            to_sib(s, offs[i], 2)

    def ev_f(s):
        await_(xx.at[o, s], sib_sem.at[s])
        start = pl.multiple_of(y * (4 * rows), 16)
        for a in range(2):
            pltpu.make_async_copy(
                xx.at[a, s, pl.ds(start, 4 * rows), :],
                own_hbm.at[a, :, pl.ds(s * toks, toks)],
                own_sem.at[a, s],
            ).start()

    def y_send():
        b = blk(0, 0, 0)
        rput(b, blk(1, 0, 0), misc_send.at[1], y_sem.at[0], y_p)
        rput(b, blk(2, 0, 0), misc_send.at[1], y_sem.at[1], y_m)
        rput(prefix_in, levels.at[1], misc_send.at[2], lev_sem.at[0], y_p)
        rput(prefix_in, levels.at[2], misc_send.at[2], lev_sem.at[1], y_m)

    def y_forward():
        rput(blk(1, 0, 0, 0, TOP), blk(3, 0, 0, 0, TOP), misc_send.at[1], y_sem.at[2], y_p)
        rput(blk(2, 0, 0, TOP, rest), blk(3, 0, 0, TOP, rest), misc_send.at[1], y_sem.at[3], y_m)
        await_(levels.at[1], lev_sem.at[0])
        await_(levels.at[2], lev_sem.at[1])
        rput(levels.at[1], levels.at[3], misc_send.at[2], lev_sem.at[2], y_p)

    def gate_step(s):
        gate_f[...] = contract(xx[0, s], gate_w[...], 0, 0)

    def up_step(s):
        up_f[...] = contract(xx[0, s], up_w[...], 0, 0)

    def back_step(s):
        back_f[...] = contract(xx[1, s], down_w[...], 0, 1)

    def act_copy(s):
        return pltpu.make_async_copy(
            acts.at[s % 2], acts_hbm.at[:, pl.ds(s * toks, toks), :], act_sem.at[s]
        )

    def point_step(s):
        local = gate_w.shape[1]
        if s == 3:
            await_(levels.at[3], lev_sem.at[2])
        if s >= 2:
            act_copy(s - 2).wait()
        width = jnp.left_shift(jnp.full(levels.shape[1:], UNIT, jnp.int32), levels[s])
        mask = jnp.where(c * local < width, 1.0, 0.0).astype(F32)
        for b in range(toks // BLOCK):
            keep = jnp.broadcast_to(mask[b : b + 1, 0:1], (16, local))

            @pl.loop(0, BLOCK // 16)
            def _(k):
                r = pl.ds(pl.multiple_of(b * BLOCK + k * 16, 16), 16)
                act, slope = gelu_pair(gate_f[r, :])
                up = up_f[r, :] * keep
                back = back_f[r, :] * keep
                acts[s % 2, 2, r, :] = (act * up).astype(BF)
                acts[s % 2, 0, r, :] = (back * up * slope).astype(BF)
                acts[s % 2, 1, r, :] = (back * act).astype(BF)

        act_copy(s).start()

    third = xx.shape[2] // 3

    def out_step(t):
        part[0, pl.ds(t * third, third), :] = contract(
            down_w[:, pl.ds(t * third, third)], acts[0, 2], 0, 1
        ).astype(BF)

    def toward_step(t):
        r = pl.ds(t * third, third)
        part[1, r, :] = (
            contract(gate_w[r, :], acts[0, 0], 1, 1) + contract(up_w[r, :], acts[0, 1], 1, 1)
        ).astype(BF)

    def rs_0():
        rput(part.at[o], part_sib, misc_send.at[3], rs_sem.at[0], sib)

    def add_into(start, n, other):
        r = pl.ds(pl.multiple_of(start, 16), n)
        part[h, r, :] = (part[h, r, :].astype(F32) + other.astype(F32)).astype(BF)

    def pblk(d1, d2, lo=0, n=None):
        return part.at[h, pl.ds(row(d1, d2) + lo, rows if n is None else n), :]

    def rs_1():
        await_(part_sib, rs_sem.at[0])

        @pl.loop(0, 16)
        def _(k):
            start = k * rows
            add_into(start, rows, part_sib[pl.ds(pl.multiple_of(start, 16), rows), :])

        for j, i in enumerate((0, 2)):
            rput(pblk(offs[i], 2), line_two.at[0, j], misc_send.at[4], rs_sem.at[1 + j], two_p)
        for j, i in enumerate((1, 3)):
            rput(pblk(offs[i], 2), line_two.at[1, j], misc_send.at[4], rs_sem.at[3 + j], two_m)

    def rs_2():
        for j, i in enumerate((0, 2)):
            await_(line_two.at[0, j], rs_sem.at[1 + j])
            add_into(row(offs[i], 1), rows, line_two[0, j])
        for j, i in enumerate((1, 3)):
            await_(line_two.at[1, j], rs_sem.at[3 + j])
            add_into(row(offs[i], -1), rows, line_two[1, j])
        for i in range(4):
            rput(pblk(offs[i], 1), line_four.at[0, i], misc_send.at[5], rs_sem.at[5 + i], two_p)
            rput(pblk(offs[i], -1), line_four.at[1, i], misc_send.at[5], rs_sem.at[9 + i], two_m)

    def rs_3():
        for i in range(4):
            await_(line_four.at[0, i], rs_sem.at[5 + i])
            await_(line_four.at[1, i], rs_sem.at[9 + i])
            both = line_four[0, i].astype(F32) + line_four[1, i].astype(F32)
            add_into(row(offs[i], 0), rows, both)
        rput(
            pblk(2, 0, 0, TOP), block_half.at[pl.ds(0, TOP), :], misc_send.at[6], rs_sem.at[13], one_p
        )
        rput(
            pblk(2, 0, TOP, rest),
            block_half.at[pl.ds(TOP, rest), :],
            misc_send.at[6],
            rs_sem.at[14],
            one_m,
        )

    def rs_4():
        await_(block_half.at[pl.ds(0, TOP), :], rs_sem.at[13])
        add_into(row(1, 0), TOP, block_half[0:TOP, :])
        await_(block_half.at[pl.ds(TOP, rest), :], rs_sem.at[14])
        add_into(row(-1, 0) + TOP, rest, block_half[TOP:rows, :])
        rput(pblk(1, 0), block_one.at[0], misc_send.at[7], rs_sem.at[15], one_p)
        rput(pblk(-1, 0), block_one.at[1], misc_send.at[7], rs_sem.at[16], one_m)

    def rs_5():
        await_(block_one.at[0], rs_sem.at[15])
        await_(block_one.at[1], rs_sem.at[16])
        total = (
            part[h, pl.ds(row(0, 0), rows), :].astype(F32)
            + block_one[0].astype(F32)
            + block_one[1].astype(F32)
        )
        fin[0] = total[: rows // 2]
        fin[1] = total[rows // 2 :]
        rput(fin.at[o], fin_sib, misc_send.at[8], rs_sem.at[17], sib)

    def rs_6():
        await_(fin_sib, rs_sem.at[17])
        result[h] = fin[h]
        result[o] = fin_sib[...]

    ev_a(0)
    y_send()
    ev_b(0)
    ev_c(0)
    ev_d(0)
    ev_a(1)
    ev_a(2)
    y_forward()
    ev_e(0)
    ev_b(1)
    ev_f(0)
    loads[0].wait()
    gate_step(0)
    ev_c(1)
    loads[1].wait()
    up_step(0)
    ev_d(1)
    ev_b(2)
    loads[2].wait()
    back_step(0)
    ev_e(1)
    ev_c(2)
    point_step(0)
    ev_a(3)
    for t in range(3):
        out_step(t)
    ev_d(2)
    ev_b(3)
    for t in range(3):
        toward_step(t)
    ev_e(2)
    ev_c(3)
    rs_0()
    ev_f(1)
    gate_step(1)
    ev_d(3)
    rs_1()
    up_step(1)
    rs_2()
    back_step(1)
    ev_e(3)
    point_step(1)
    ev_f(2)
    gate_step(2)
    rs_3()
    up_step(2)
    rs_4()
    back_step(2)
    rs_5()
    point_step(2)
    ev_f(3)
    gate_step(3)
    rs_6()
    up_step(3)
    back_step(3)
    point_step(3)

    act_copy(2).wait()
    act_copy(3).wait()
    for s in range(4):
        for a in range(2):
            pltpu.make_async_copy(
                xx.at[a, s, pl.ds(0, 4 * rows), :],
                own_hbm.at[a, :, pl.ds(s * toks, toks)],
                own_sem.at[a, s],
            ).wait()
        await_(xx.at[0, s, pl.ds(0, 15 * rows), :], send_sem.at[s])
        await_(xx.at[0, s], sib_send_sem.at[s])
    await_(z_in, misc_send.at[0])
    await_(xx.at[0, 0, pl.ds(0, 3 * rows), :], misc_send.at[1])
    await_(levels.at[pl.ds(0, 3)], misc_send.at[2])
    await_(part_sib, misc_send.at[3])
    await_(line_two, misc_send.at[4])
    await_(line_four, misc_send.at[5])
    await_(block_half, misc_send.at[6])
    await_(block_one, misc_send.at[7])
    await_(fin_sib, misc_send.at[8])


def layer(z, levels, gate_weight, up_weight, down_weight):
    _, feats, toks = z.shape
    width, local = gate_weight.shape
    rows = 2 * feats
    dma = pltpu.SemaphoreType.DMA
    any_ = pl.BlockSpec(memory_space=pltpu.HBM)
    vmem = pl.BlockSpec(memory_space=pltpu.VMEM)
    return pl.pallas_call(
        layer_kernel,
        out_shape=(
            jax.ShapeDtypeStruct((3, 4 * toks, local), BF),
            jax.ShapeDtypeStruct((2, 4 * rows, 4 * toks), BF),
            jax.ShapeDtypeStruct((2, feats, toks), F32),
        ),
        in_specs=[vmem, vmem, any_, any_, any_],
        out_specs=(any_, any_, vmem),
        scratch_shapes=[
            pltpu.VMEM((width, local), BF),
            pltpu.VMEM((width, local), BF),
            pltpu.VMEM((local, width), BF),
            pltpu.VMEM((2, 4, width, toks), BF),
            pltpu.VMEM((2, feats, toks), BF),
            pltpu.VMEM((4, 8, 128), jnp.int32),
            pltpu.VMEM((toks, local), F32),
            pltpu.VMEM((toks, local), F32),
            pltpu.VMEM((toks, local), F32),
            pltpu.VMEM((2, 3, toks, local), BF),
            pltpu.VMEM((2, width, toks), BF),
            pltpu.VMEM((width, toks), BF),
            pltpu.VMEM((2, 2, rows, toks), BF),
            pltpu.VMEM((2, 4, rows, toks), BF),
            pltpu.VMEM((rows, toks), BF),
            pltpu.VMEM((2, rows, toks), BF),
            pltpu.VMEM((2, feats, toks), F32),
            pltpu.VMEM((feats, toks), F32),
            dma((3,)),
            dma((1,)),
            dma((3,)),
            dma((4,)),
            dma((4, 4)),
            dma((4, 12)),
            dma((4,)),
            dma((4,)),
            dma((4,)),
            dma((9,)),
            dma((18,)),
            dma((4,)),
            dma((2, 4)),
        ],
        compiler_params=pltpu.CompilerParams(
            collective_id=0, has_side_effects=True, vmem_limit_bytes=67043328
        ),
        name="layer",
    )(z, levels, gate_weight, up_weight, down_weight)


def grads_kernel(own, acts, gate_out, up_out, down_out):
    which = pl.program_id(0)
    value = jnp.dot(own[0], acts[0], preferred_element_type=F32)

    @pl.when(which == 0)
    def _():
        gate_out[...] = value.astype(BF)

    @pl.when(which == 1)
    def _():
        up_out[...] = value.astype(BF)

    @pl.when(which == 2)
    def _():
        down_out[...] = value.T.astype(BF)


def weight_grads(acts, own):
    _, toks, local = acts.shape
    feats = own.shape[1]
    tile = 384
    last = local // tile - 1
    return pl.pallas_call(
        grads_kernel,
        grid=(3, local // tile),
        out_shape=(
            jax.ShapeDtypeStruct((feats, local), BF),
            jax.ShapeDtypeStruct((feats, local), BF),
            jax.ShapeDtypeStruct((local, feats), BF),
        ),
        in_specs=[
            pl.BlockSpec((1, feats, toks), lambda a, n: (a // 2, 0, 0)),
            pl.BlockSpec((1, toks, tile), lambda a, n: (a, 0, n)),
        ],
        out_specs=(
            pl.BlockSpec((feats, tile), lambda a, n: (0, jnp.where(a == 0, n, last))),
            pl.BlockSpec((feats, tile), lambda a, n: (0, jnp.where(a == 1, n, jnp.where(a < 1, 0, last)))),
            pl.BlockSpec((tile, feats), lambda a, n: (jnp.where(a == 2, n, 0), 0)),
        ),
        compiler_params=pltpu.CompilerParams(vmem_limit_bytes=48 * 2**20),
        name="weight_grads",
    )(own, acts)


def body(tokens, cotangent, prefix, gate_weight, up_weight, down_weight):
    z = jnp.stack([tokens.T, cotangent.T])
    blocks = prefix.shape[0]
    levels = jnp.broadcast_to(jnp.pad(prefix, (0, 8 - blocks))[:, None], (8, 128))
    acts, own, result = layer(z, levels, gate_weight, up_weight, down_weight)
    grad_gate, grad_up, grad_down = weight_grads(acts, own)
    return (
        result[0].T.astype(BF),
        result[1].T.astype(BF),
        grad_gate,
        grad_up,
        grad_down,
    )


def solution(mesh):
    return jax.shard_map(
        body,
        mesh=mesh,
        in_specs=(
            P("dp", "col"),
            P("dp", "col"),
            P("dp"),
            P(None, "col"),
            P(None, "col"),
            P("col", None),
        ),
        out_specs=(P("dp", "col"), P("dp", "col"), P("dp", "col"), P("dp", "col"), P("col", "dp")),
        check_vma=False,
    )
```

time: 274 us -> 119 us (0.43)
  Pallas kernels: 0 us -> 109 us
  waiting for transfers between devices: 93.8 us -> 0 us
  matrix products: 47.9 us -> 0 us
  local copies, waits for them, and re-layouts: 52.9 us -> 5.72 us
  blocking collectives: 29 us -> 0 us
  other arithmetic: 21.4 us -> 2.45 us
  between operations: 14.2 us -> 0.65 us
  starting transfers between devices: 13 us -> 0 us
    pallas_call x0 -> x2, Pallas kernels: none -> 109 us  [the longest x1 95.7 us: layer(): pl.pallas_call(layer_kernel, out_shape=(jax.ShapeDtypeStruct((3, 4 * toks...]
    all_gather x2 -> x0, waiting for transfers between devices: 48.2 us -> none  [the longest x1 46.8 us: rows_first(): whole = lax.all_gather(both, axis, axis=0, tiled=True)]
    dot_general x8 -> x0, matrix products: 47.9 us -> none  [the longest x3 14.2 us: contract_last(): lax.dot_general(left, right, (((1,), (1,)), ((), ())), preferred_element_...]
    all_to_all x3 -> x0, waiting for transfers between devices: 45.5 us -> none  [the longest x1 31.7 us: body(): lax.all_to_all(grad_out, 'dp', split_axis=1, concat_axis=0, tiled=True)]
    all_to_all x1 -> x0, blocking collectives: 29 us -> none  [summed_on_arrival(): lax.all_to_all(blocks, axis, split_axis=0, concat_axis=0, tiled=True)]
    all_gather x1 -> x0, local copies, waits for them, and re-layouts: 13.6 us -> none  [one_gather(): lines, at, finished = (lax.all_gather(ravelled, axis), 0, [])]
    all_to_all x3 -> x0, starting transfers between devices: 12.9 us -> none  [the longest x1 4.62 us: body(): lax.all_to_all(whole, 'dp', split_axis=1, concat_axis=0, tiled=True)]
    reduce_sum x3 -> x0, other arithmetic: 12 us -> none  [the longest x1 10.2 us: body(): summed = jnp.sum(stacked.astype(jnp.bfloat16).astype(jnp.float32), axis=0)]
  transfers between devices with their start and end apart: 5 -> 0, of which waited for: 4 -> 0; matrix products, arithmetic and copies ran while one was open for 21% -> 0% of each run, Pallas kernels for 0% -> 0%
where the time goes in v1:
time: 119 us; the launch traced here: 118 us
  Pallas kernels  109 us (92%)
  local copies, waits for them, and re-layouts  5.72 us (5%)
  other arithmetic  2.45 us (2%)
    pallas_call x1, Pallas kernels, layer(): pl.pallas_call(layer_kernel, out_shape=(jax.ShapeDtypeStruct((3, 4 * toks...  95.7 us
    pallas_call x1, Pallas kernels, weight_grads(): pl.pallas_call(grads_kernel, grid=(3, local // tile), out_shape=(jax.Shap...  13.8 us
    unnamed x3, local copies, waits for them, and re-layouts  3.75 us

profile of v1, /device:TPU:0, one launch (start us, length us, event | category | flops | bytes accessed | tf_op | source)
XLA Modules:
  0.0 118.3 jit_solution(3215951526475630322)
XLA Ops:
  0.6 0.7 pad.4
  1.3 0.7 broadcast_in_dim.2.prefix_in
  2.0 1.5 %pad_maximum_fusion.z_in = bf16[2,72,384]{2,1,0:T(8,128)(2,1)} fusion(bf16[1,72,384]{2,1,0:T(8,128)(2,1)} %bitcast.14, bf16[1,72,384]{2,1,0:T(8,128)(2,1)} %bitcast.15), kind=kLoop, calls=%fused_computation | loop fusion | flops 55296 | bytes 221184 | tf_op jit(solution)/shard_map/stack | solution.py:531
  3.5 95.7 %layer.1 = (bf16[3,1536,1152]{2,1,0:T(8,128)(2,1)}, bf16[2,576,1536]{2,1,0:T(8,128)(2,1)}, f32[2,72,384]{2,1,0:T(8,128)}) custom-call(bf16[2,72,384]{2,1,0:T(8,128)(2,1)} %pad_maximum_fusion.z_in, s32[8,128]{1,0:T(8,128)} %broadcast_in_dim.2.prefix_in, bf16[2304,1152]{1,0:T(8,128)(2,1)} %gate_hbm.1, bf16[2304,1152]{1,0:T(8,128)(2,1)} %up_hbm.1, ...), custom_call_target="tpu_custom_call" | custom-call | tf_op jit(solution)/shard_map/layer/pallas_call | solution.py:437
  99.1 1.0 convert.4
  100.1 0.6 slice_bitcast_fusion
  100.7 0.0 copy-start
  100.7 2.0 %copy-done = bf16[2,576,1536]{2,1,0:T(8,128)(2,1)S(1)} copy-done((bf16[2,576,1536]{2,1,0:T(8,128)(2,1)S(1)}, bf16[2,576,1536]{2,1,0:T(8,128)(2,1)}, u32[]{:S(2)}) %copy-start) | copy-done | bytes 3538968
  102.7 13.8 %weight_grads.1 = (bf16[576,1152]{1,0:T(8,128)(2,1)}, bf16[576,1152]{1,0:T(8,128)(2,1)}, bf16[1152,576]{1,0:T(8,128)(2,1)S(1)}) custom-call(bf16[2,576,1536]{2,1,0:T(8,128)(2,1)S(1)} %copy-done, bf16[3,1536,1152]{2,1,0:T(8,128)(2,1)} %get-tuple-element.13.acts), custom_call_target="tpu_custom_call" | custom-call | tf_op jit(solution)/shard_map/weight_grads/pallas_call | solution.py:508
  116.5 1.7 %copy.11 = bf16[1152,576]{0,1:T(8,128)(2,1)} copy(bf16[1152,576]{1,0:T(8,128)(2,1)S(1)} %get-tuple-element.21) | data formatting | bytes 2654208
Async XLA Ops:
  100.7 2.0 %copy-start = (bf16[2,576,1536]{2,1,0:T(8,128)(2,1)S(1)}, bf16[2,576,1536]{2,1,0:T(8,128)(2,1)}, u32[]{:S(2)}) copy-start(bf16[2,576,1536]{2,1,0:T(8,128)(2,1)} %get-tuple-element.12.own) | copy-start | bytes 10616836

commit v2 on v1

--- a/solution.py
+++ b/solution.py
@@ -34,14 +34,16 @@
 
 
 def layer_kernel(
-    z_in,
+    tokens_in,
+    cotangent_in,
     prefix_in,
     gate_hbm,
     up_hbm,
     down_hbm,
     acts_hbm,
     own_hbm,
-    result,
+    out_ref,
+    grad_ref,
     gate_w,
     up_w,
     down_w,
@@ -74,8 +76,8 @@
     act_sem,
     own_sem,
 ):
-    toks = z_in.shape[2]
-    rows = 2 * z_in.shape[1]
+    feats, toks = tokens_in.shape
+    rows = 2 * feats
     y = lax.axis_index("dp")
     c = lax.axis_index("col")
     h = lax.rem(c, 2)
@@ -124,10 +126,17 @@
         pl.semaphore_signal(barrier, inc=1, device_id=to, device_id_type=MESH)
     pl.semaphore_wait(barrier, 7)
 
-    rput(z_in, z_sib, misc_send.at[0], z_sem.at[0], sib)
-    levels[0] = prefix_in[...]
-    await_(z_sib, z_sem.at[0])
-    mine, other = z_in[h].astype(F32), z_sib[h].astype(F32)
+    rput(tokens_in, z_sib.at[0], misc_send.at[0], z_sem.at[0], sib)
+    rput(cotangent_in, z_sib.at[1], misc_send.at[0], z_sem.at[1], sib)
+    which = lax.broadcasted_iota(jnp.int32, levels.shape[1:], 0)
+    level = jnp.full(levels.shape[1:], prefix_in[0], jnp.int32)
+    for b in range(1, prefix_in.shape[0]):
+        level = jnp.where(which == b, prefix_in[b], level)
+    levels[0] = level
+    await_(z_sib.at[0], z_sem.at[0])
+    await_(z_sib.at[1], z_sem.at[1])
+    mine = jnp.where(h == 0, tokens_in[...].astype(F32), cotangent_in[...].astype(F32))
+    other = z_sib[h].astype(F32)
     low = jnp.where(h == 0, mine, other)
     high = jnp.where(h == 0, other, mine)
     xx[h, 0, pl.ds(row(0, 0), rows), :] = jnp.concatenate([low, high], axis=0).astype(BF)
@@ -136,9 +145,18 @@
     offs = (0, -1, 1, 2)
 
     def to_sib(s, d1, d2):
-        rput(blk(s, d1, d2), blk(s, d1, d2), sib_send_sem.at[s], sib_sem.at[s], sib)
+        b = blk(s, d1, d2)
+        rput(b, b, sib_send_sem.at[s], sib_sem.at[s, d2 % 4], sib)
+
+    def over_y(i, d1, d2):
+        for slot, to in ((1, y_p), (2, y_m)):
+            rput(
+                blk(0, d1, d2), blk(slot, d1, d2), misc_send.at[9], two_sem.at[slot, i], to
+            )
 
     def across(s, i):
+        if s in (1, 2) and i == 3:
+            return
         d1 = offs[i]
         b = blk(s, d1, 0)
         rput(b, b, send_sem.at[s], two_sem.at[s, i], two_p)
@@ -156,50 +174,70 @@
         across(s, 0)
         to_sib(s, 0, 0)
 
-    def ev_b(s):
+    def ev_b1(s):
         await_(blk(s, -1, 0), one_sem.at[s, 0])
         b = blk(s, -1, 0, 0, TOP)
         rput(b, b, send_sem.at[s], one_sem.at[s, 2], one_p)
+        across(s, 1)
+        to_sib(s, -1, 0)
+
+    def ev_b2(s):
         await_(blk(s, 1, 0), one_sem.at[s, 1])
         b = blk(s, 1, 0, TOP, rest)
         rput(b, b, send_sem.at[s], one_sem.at[s, 3], one_m)
-        across(s, 1)
         across(s, 2)
-        to_sib(s, -1, 0)
         to_sib(s, 1, 0)
 
-    def from_two(s, i):
-        d1 = offs[i]
-        await_(blk(s, d1, -1), two_sem.at[s, i])
-        if i in (0, 2):
-            b = blk(s, d1, -1)
-            rput(b, b, send_sem.at[s], two_sem.at[s, 8 + i], two_p)
-        to_sib(s, d1, -1)
-        await_(blk(s, d1, 1), two_sem.at[s, 4 + i])
-        if i in (1, 3):
-            b = blk(s, d1, 1)
-            rput(b, b, send_sem.at[s], two_sem.at[s, 8 + i], two_m)
-        to_sib(s, d1, 1)
-
     def ev_c(s):
-        from_two(s, 0)
         await_(blk(s, 2, 0, 0, TOP), one_sem.at[s, 2])
         await_(blk(s, 2, 0, TOP, rest), one_sem.at[s, 3])
         across(s, 3)
         to_sib(s, 2, 0)
 
-    def ev_d(s):
-        from_two(s, 1)
-        from_two(s, 2)
-        from_two(s, 3)
-
-    def ev_e(s):
-        for i in range(4):
-            await_(blk(s, offs[i], 2), two_sem.at[s, 8 + i])
-            to_sib(s, offs[i], 2)
+    def ev_m(s, i):
+        b = blk(s, offs[i], -1)
+        await_(b, two_sem.at[s, i])
+        if i in (0, 2) and s in (0, 3):
+            rput(b, b, send_sem.at[s], two_sem.at[s, 8 + i], two_p)
+        to_sib(s, offs[i], -1)
+        if i == 3 and s == 0:
+            over_y(i, offs[i], -1)
+
+    def ev_p(s, i):
+        b = blk(s, offs[i], 1)
+        await_(b, two_sem.at[s, 4 + i])
+        if i in (1, 3) and s in (0, 3):
+            rput(b, b, send_sem.at[s], two_sem.at[s, 8 + i], two_m)
+        to_sib(s, offs[i], 1)
+        if i == 3 and s == 0:
+            over_y(4 + i, offs[i], 1)
+
+    def ev_e(s, i):
+        await_(blk(s, offs[i], 2), two_sem.at[s, 8 + i])
+        to_sib(s, offs[i], 2)
+        if s == 0:
+            over_y(8 + i, offs[i], 2)
+
+    def await_line(s, k):
+        await_(xx.at[o, s, pl.ds(0, 4 * rows), :], sib_sem.at[s, k])
+
+    def chunk_step(k):
+        d2 = (0, -1, 1, 2)[k]
+        await_line(0, d2 % 4)
+        r = pl.ds(pl.multiple_of(lax.rem(zc + d2 % 4, 4) * (4 * rows), 16), 4 * rows)
+        gate = contract(xx[0, 0, r, :], gate_w[r, :], 0, 0)
+        up = contract(xx[0, 0, r, :], up_w[r, :], 0, 0)
+        if k == 0:
+            gate_f[...] = gate
+            up_f[...] = up
+        else:
+            gate_f[...] += gate
+            up_f[...] += up
 
     def ev_f(s):
-        await_(xx.at[o, s], sib_sem.at[s])
+        if s > 0:
+            for k in range(4):
+                await_line(s, k)
         start = pl.multiple_of(y * (4 * rows), 16)
         for a in range(2):
             pltpu.make_async_copy(
@@ -212,8 +250,8 @@
         b = blk(0, 0, 0)
         rput(b, blk(1, 0, 0), misc_send.at[1], y_sem.at[0], y_p)
         rput(b, blk(2, 0, 0), misc_send.at[1], y_sem.at[1], y_m)
-        rput(prefix_in, levels.at[1], misc_send.at[2], lev_sem.at[0], y_p)
-        rput(prefix_in, levels.at[2], misc_send.at[2], lev_sem.at[1], y_m)
+        rput(levels.at[0], levels.at[1], misc_send.at[2], lev_sem.at[0], y_p)
+        rput(levels.at[0], levels.at[2], misc_send.at[2], lev_sem.at[1], y_m)
 
     def y_forward():
         rput(blk(1, 0, 0, 0, TOP), blk(3, 0, 0, 0, TOP), misc_send.at[1], y_sem.at[2], y_p)
@@ -236,28 +274,28 @@
             acts.at[s % 2], acts_hbm.at[:, pl.ds(s * toks, toks), :], act_sem.at[s]
         )
 
-    def point_step(s):
+    def point_step(s, b):
         local = gate_w.shape[1]
-        if s == 3:
+        if s == 3 and b == 0:
             await_(levels.at[3], lev_sem.at[2])
-        if s >= 2:
+        if s >= 2 and b == 0:
             act_copy(s - 2).wait()
         width = jnp.left_shift(jnp.full(levels.shape[1:], UNIT, jnp.int32), levels[s])
         mask = jnp.where(c * local < width, 1.0, 0.0).astype(F32)
-        for b in range(toks // BLOCK):
-            keep = jnp.broadcast_to(mask[b : b + 1, 0:1], (16, local))
-
-            @pl.loop(0, BLOCK // 16)
-            def _(k):
-                r = pl.ds(pl.multiple_of(b * BLOCK + k * 16, 16), 16)
-                act, slope = gelu_pair(gate_f[r, :])
-                up = up_f[r, :] * keep
-                back = back_f[r, :] * keep
-                acts[s % 2, 2, r, :] = (act * up).astype(BF)
-                acts[s % 2, 0, r, :] = (back * up * slope).astype(BF)
-                acts[s % 2, 1, r, :] = (back * act).astype(BF)
-
-        act_copy(s).start()
+        keep = jnp.broadcast_to(mask[b : b + 1, 0:1], (16, local))
+
+        @pl.loop(0, BLOCK // 16)
+        def _(k):
+            r = pl.ds(pl.multiple_of(b * BLOCK + k * 16, 16), 16)
+            act, slope = gelu_pair(gate_f[r, :])
+            up = up_f[r, :] * keep
+            back = back_f[r, :] * keep
+            acts[s % 2, 2, r, :] = (act * up).astype(BF)
+            acts[s % 2, 0, r, :] = (back * up * slope).astype(BF)
+            acts[s % 2, 1, r, :] = (back * act).astype(BF)
+
+        if b == toks // BLOCK - 1:
+            act_copy(s).start()
 
     third = xx.shape[2] // 3
 
@@ -345,66 +383,122 @@
 
     def rs_6():
         await_(fin_sib, rs_sem.at[17])
-        result[h] = fin[h]
-        result[o] = fin_sib[...]
+        mine, other = fin[h], fin_sib[...]
+        out_ref[...] = jnp.where(h == 0, mine, other).astype(BF)
+        grad_ref[...] = jnp.where(h == 0, other, mine).astype(BF)
 
     ev_a(0)
     y_send()
-    ev_b(0)
+    ev_m(0, 0)
+    ev_b2(0)
+    ev_b1(0)
     ev_c(0)
-    ev_d(0)
+    ev_p(0, 0)
+    ev_p(0, 2)
+    ev_e(0, 0)
+    ev_p(0, 1)
+    ev_m(0, 2)
+    ev_p(0, 3)
     ev_a(1)
+    ev_m(0, 1)
     ev_a(2)
     y_forward()
-    ev_e(0)
-    ev_b(1)
+    loads[0].wait()
+    loads[1].wait()
+    chunk_step(0)
+    ev_m(0, 3)
+    chunk_step(1)
+    ev_e(0, 2)
+    ev_e(0, 3)
+    ev_b2(1)
+    ev_e(0, 1)
+    chunk_step(2)
+    chunk_step(3)
+    ev_a(3)
+    ev_b1(1)
     ev_f(0)
-    loads[0].wait()
-    gate_step(0)
-    ev_c(1)
-    loads[1].wait()
-    up_step(0)
-    ev_d(1)
-    ev_b(2)
     loads[2].wait()
     back_step(0)
-    ev_e(1)
-    ev_c(2)
-    point_step(0)
-    ev_a(3)
-    for t in range(3):
-        out_step(t)
-    ev_d(2)
-    ev_b(3)
-    for t in range(3):
-        toward_step(t)
-    ev_e(2)
-    ev_c(3)
+    ev_e(2, 0)
+    point_step(0, 0)
+    ev_p(2, 3)
+    point_step(0, 1)
+    point_step(0, 2)
+    out_step(0)
+    ev_m(1, 3)
+    ev_p(1, 0)
+    out_step(1)
+    out_step(2)
+    ev_b1(2)
+    ev_b2(3)
+    ev_b2(2)
+    ev_p(1, 3)
+    toward_step(0)
+    ev_m(2, 3)
+    ev_c(1)
+    ev_e(1, 0)
+    ev_b1(3)
+    ev_m(2, 0)
+    ev_p(1, 2)
+    ev_e(2, 2)
+    toward_step(1)
+    ev_p(1, 1)
+    ev_e(1, 2)
+    ev_e(1, 3)
+    ev_m(1, 2)
+    ev_m(1, 0)
+    ev_m(1, 1)
+    toward_step(2)
+    ev_e(1, 1)
     rs_0()
     ev_f(1)
+    ev_c(3)
     gate_step(1)
-    ev_d(3)
     rs_1()
+    ev_c(2)
+    ev_p(3, 1)
     up_step(1)
+    ev_e(2, 1)
+    ev_p(2, 0)
+    ev_p(2, 2)
+    ev_m(2, 2)
+    ev_m(2, 1)
+    ev_m(3, 0)
+    ev_m(3, 2)
+    ev_p(2, 1)
+    ev_p(3, 3)
+    back_step(1)
+    ev_e(2, 3)
+    ev_m(3, 1)
+    point_step(1, 0)
+    point_step(1, 1)
     rs_2()
-    back_step(1)
-    ev_e(3)
-    point_step(1)
+    ev_m(3, 3)
+    point_step(1, 2)
     ev_f(2)
     gate_step(2)
+    up_step(2)
+    ev_e(3, 0)
+    ev_e(3, 3)
+    back_step(2)
+    ev_e(3, 2)
+    ev_e(3, 1)
+    ev_p(3, 2)
+    ev_p(3, 0)
+    point_step(2, 0)
+    point_step(2, 1)
     rs_3()
-    up_step(2)
-    rs_4()
-    back_step(2)
-    rs_5()
-    point_step(2)
+    point_step(2, 2)
     ev_f(3)
     gate_step(3)
-    rs_6()
+    rs_4()
     up_step(3)
     back_step(3)
-    point_step(3)
-
+    rs_5()
+    point_step(3, 0)
+    point_step(3, 1)
+    point_step(3, 2)
+    rs_6()
     act_copy(2).wait()
     act_copy(3).wait()
     for s in range(4):
@@ -414,9 +508,10 @@
                 own_hbm.at[a, :, pl.ds(s * toks, toks)],
                 own_sem.at[a, s],
             ).wait()
-        await_(xx.at[0, s, pl.ds(0, 15 * rows), :], send_sem.at[s])
+        sent = 15 if s in (0, 3) else 9
+        await_(xx.at[0, s, pl.ds(0, sent * rows), :], send_sem.at[s])
         await_(xx.at[0, s], sib_send_sem.at[s])
-    await_(z_in, misc_send.at[0])
+    await_(z_sib, misc_send.at[0])
     await_(xx.at[0, 0, pl.ds(0, 3 * rows), :], misc_send.at[1])
     await_(levels.at[pl.ds(0, 3)], misc_send.at[2])
     await_(part_sib, misc_send.at[3])
@@ -425,10 +520,11 @@
     await_(block_half, misc_send.at[6])
     await_(block_one, misc_send.at[7])
     await_(fin_sib, misc_send.at[8])
-
-
-def layer(z, levels, gate_weight, up_weight, down_weight):
-    _, feats, toks = z.shape
+    await_(xx.at[0, 0, pl.ds(0, 12 * rows), :], misc_send.at[9])
+
+
+def layer(tokens, cotangent, prefix, gate_weight, up_weight, down_weight):
+    feats, toks = tokens.shape
     width, local = gate_weight.shape
     rows = 2 * feats
     dma = pltpu.SemaphoreType.DMA
@@ -439,10 +535,11 @@
         out_shape=(
             jax.ShapeDtypeStruct((3, 4 * toks, local), BF),
             jax.ShapeDtypeStruct((2, 4 * rows, 4 * toks), BF),
-            jax.ShapeDtypeStruct((2, feats, toks), F32),
+            jax.ShapeDtypeStruct((feats, toks), BF),
+            jax.ShapeDtypeStruct((feats, toks), BF),
         ),
-        in_specs=[vmem, vmem, any_, any_, any_],
-        out_specs=(any_, any_, vmem),
+        in_specs=[vmem, vmem, pl.BlockSpec(memory_space=pltpu.SMEM), any_, any_, any_],
+        out_specs=(any_, any_, vmem, vmem),
         scratch_shapes=[
             pltpu.VMEM((width, local), BF),
             pltpu.VMEM((width, local), BF),
@@ -463,15 +560,15 @@
             pltpu.VMEM((2, feats, toks), F32),
             pltpu.VMEM((feats, toks), F32),
             dma((3,)),
-            dma((1,)),
+            dma((2,)),
             dma((3,)),
             dma((4,)),
             dma((4, 4)),
             dma((4, 12)),
+            dma((4, 4)),
             dma((4,)),
             dma((4,)),
-            dma((4,)),
-            dma((9,)),
+            dma((10,)),
             dma((18,)),
             dma((4,)),
             dma((2, 4)),
@@ -480,66 +577,122 @@
             collective_id=0, has_side_effects=True, vmem_limit_bytes=67043328
         ),
         name="layer",
-    )(z, levels, gate_weight, up_weight, down_weight)
-
-
-def grads_kernel(own, acts, gate_out, up_out, down_out):
-    which = pl.program_id(0)
-    value = jnp.dot(own[0], acts[0], preferred_element_type=F32)
-
-    @pl.when(which == 0)
-    def _():
-        gate_out[...] = value.astype(BF)
-
-    @pl.when(which == 1)
-    def _():
-        up_out[...] = value.astype(BF)
-
-    @pl.when(which == 2)
-    def _():
-        down_out[...] = value.T.astype(BF)
-
-
-def weight_grads(acts, own):
-    _, toks, local = acts.shape
+    )(tokens, cotangent, prefix, gate_weight, up_weight, down_weight)
+
+
+def grads_kernel(
+    own_hbm,
+    acts_hbm,
+    first_hbm,
+    second_hbm,
+    gate_out,
+    up_out,
+    down_out,
+    first_out,
+    second_out,
+    own,
+    acts,
+    done,
+    small,
+    in_sem,
+    out_sem,
+    small_sem,
+):
+    half = own.shape[2] // 2
+    halves = (pl.ds(0, half), pl.ds(half, half))
+
+    def own_load(a, j):
+        return pltpu.make_async_copy(
+            own_hbm.at[a, :, halves[j]], own.at[a, :, halves[j]], in_sem.at[2 * a + j]
+        )
+
+    def acts_load(k, j):
+        return pltpu.make_async_copy(
+            acts_hbm.at[k, halves[j]], acts.at[k, halves[j]], in_sem.at[4 + 2 * k + j]
+        )
+
+    for k in range(3):
+        for j in range(2):
+            if k != 1:
+                own_load(k // 2, j).start()
+            acts_load(k, j).start()
+    brought = [
+        pltpu.make_async_copy(src, small.at[j], small_sem.at[j])
+        for j, src in enumerate((first_hbm, second_hbm))
+    ]
+    taken = [
+        pltpu.make_async_copy(small.at[j], dst, small_sem.at[j])
+        for j, dst in enumerate((first_out, second_out))
+    ]
+    for copy in brought:
+        copy.start()
+    outs = (gate_out, up_out, down_out)
+    stores = [pltpu.make_async_copy(done.at[k], outs[k], out_sem.at[k]) for k in range(3)]
+
+    @pl.loop(0, 3)
+    def _(k):
+        a = k // 2
+        value = None
+        for j in range(2):
+
+            @pl.when(k != 1)
+            def _():
+                own_load(a, j).wait()
+
+            acts_load(k, j).wait()
+            term = jnp.dot(
+                own[a, :, halves[j]], acts[k, halves[j], :], preferred_element_type=F32
+            )
+            value = term if value is None else value + term
+        done[k] = value.astype(BF)
+        for i in range(3):
+
+            @pl.when(k == i)
+            def _():
+                stores[i].start()
+                if i == 0:
+                    for copy in brought:
+                        copy.wait()
+                    for copy in taken:
+                        copy.start()
+
+    for copy in stores + taken:
+        copy.wait()
+
+
+def weight_grads(acts, own, first, second):
+    kinds, toks, local = acts.shape
     feats = own.shape[1]
-    tile = 384
-    last = local // tile - 1
+    grad = jax.ShapeDtypeStruct((feats, local), BF)
+    like = jax.ShapeDtypeStruct(first.shape, BF)
+    hbm = pl.BlockSpec(memory_space=pltpu.HBM)
     return pl.pallas_call(
         grads_kernel,
-        grid=(3, local // tile),
-        out_shape=(
-            jax.ShapeDtypeStruct((feats, local), BF),
-            jax.ShapeDtypeStruct((feats, local), BF),
-            jax.ShapeDtypeStruct((local, feats), BF),
-        ),
-        in_specs=[
-            pl.BlockSpec((1, feats, toks), lambda a, n: (a // 2, 0, 0)),
-            pl.BlockSpec((1, toks, tile), lambda a, n: (a, 0, n)),
+        out_shape=(grad, grad, grad, like, like),
+        in_specs=[hbm] * 4,
+        out_specs=(hbm,) * 5,
+        scratch_shapes=[
+            pltpu.VMEM((2, feats, toks), BF),
+            pltpu.VMEM((kinds, toks, local), BF),
+            pltpu.VMEM((kinds, feats, local), BF),
+            pltpu.VMEM((2, *first.shape), BF),
+            pltpu.SemaphoreType.DMA((10,)),
+            pltpu.SemaphoreType.DMA((3,)),
+            pltpu.SemaphoreType.DMA((2,)),
         ],
-        out_specs=(
-            pl.BlockSpec((feats, tile), lambda a, n: (0, jnp.where(a == 0, n, last))),
-            pl.BlockSpec((feats, tile), lambda a, n: (0, jnp.where(a == 1, n, jnp.where(a < 1, 0, last)))),
-            pl.BlockSpec((tile, feats), lambda a, n: (jnp.where(a == 2, n, 0), 0)),
-        ),
-        compiler_params=pltpu.CompilerParams(vmem_limit_bytes=48 * 2**20),
+        compiler_params=pltpu.CompilerParams(vmem_limit_bytes=67043328),
         name="weight_grads",
-    )(own, acts)
+    )(own, acts, first, second)
 
 
 def body(tokens, cotangent, prefix, gate_weight, up_weight, down_weight):
-    z = jnp.stack([tokens.T, cotangent.T])
-    blocks = prefix.shape[0]
-    levels = jnp.broadcast_to(jnp.pad(prefix, (0, 8 - blocks))[:, None], (8, 128))
-    acts, own, result = layer(z, levels, gate_weight, up_weight, down_weight)
-    grad_gate, grad_up, grad_down = weight_grads(acts, own)
-    return (
-        result[0].T.astype(BF),
-        result[1].T.astype(BF),
-        grad_gate,
-        grad_up,
-        grad_down,
+    acts, own, output, input_grad = layer(
+        tokens.T, cotangent.T, prefix, gate_weight, up_weight, down_weight
     )
+    grad_gate, grad_up, grad_down, output, input_grad = weight_grads(
+        acts, own, output, input_grad
+    )
+    return output.T, input_grad.T, grad_gate, grad_up, grad_down.T
 
 
 def solution(mesh):

time: 119 us -> 94.3 us (0.79)
  Pallas kernels: 109 us -> 91.6 us
  local copies, waits for them, and re-layouts: 5.72 us -> 0 us
  other arithmetic: 2.45 us -> 0 us
    pallas_call x1, Pallas kernels: 95.7 us -> 80.1 us  [layer(): pl.pallas_call(layer_kernel, out_shape=(jax.ShapeDtypeStruct((3, 4 * toks...]
    unnamed x3 -> x0, local copies, waits for them, and re-layouts: 3.75 us -> none
    another operation x2 -> x0, other arithmetic: 2.45 us -> none  [the longest x1 1.5 us: body(): z = jnp.stack([tokens.T, cotangent.T])]
    pallas_call x1, Pallas kernels: 13.8 us -> 11.5 us  [weight_grads(): pl.pallas_call(grads_kernel, out_shape=(grad, grad, grad, like, like), in...]
where the time goes in v2:
time: 94.3 us; the launch traced here: 92.5 us
  Pallas kernels  91.6 us (97%)
    pallas_call x1, Pallas kernels, layer(): pl.pallas_call(layer_kernel, out_shape=(jax.ShapeDtypeStruct((3, 4 * toks...  80.1 us
    pallas_call x1, Pallas kernels, weight_grads(): pl.pallas_call(grads_kernel, out_shape=(grad, grad, grad, like, like), in...  11.5 us

profile of v2, /device:TPU:0, one launch (start us, length us, event | category | flops | bytes accessed | tf_op | source)
XLA Modules:
  0.0 92.5 jit_solution(10556057204682772072)
XLA Ops:
  0.6 80.1 %layer.1 = (bf16[3,1536,1152]{2,1,0:T(8,128)(2,1)}, bf16[2,576,1536]{2,1,0:T(8,128)(2,1)}, bf16[72,384]{1,0:T(8,128)(2,1)}, bf16[72,384]{1,0:T(8,128)(2,1)}) custom-call(bf16[72,384]{1,0:T(8,128)(2,1)} %bitcast.5, bf16[72,384]{1,0:T(8,128)(2,1)} %bitcast.6, s32[3]{0:T(128)} %prefix_in.1, bf16[2304,1152]{1,0:T(8,128)(2,1)} %gate_hbm.1, ...), custom_call_target="tpu_custom_call" | custom-call | tf_op jit(solution)/shard_map/layer/pallas_call | solution.py:533
  80.8 11.5 %weight_grads.1 = (bf16[576,1152]{1,0:T(8,128)(2,1)}, bf16[576,1152]{1,0:T(8,128)(2,1)}, bf16[576,1152]{1,0:T(8,128)(2,1)}, bf16[72,384]{1,0:T(8,128)(2,1)}, bf16[72,384]{1,0:T(8,128)(2,1)}) custom-call(bf16[2,576,1536]{2,1,0:T(8,128)(2,1)} %get-tuple-element.14.own_hbm, bf16[3,1536,1152]{2,1,0:T(8,128)(2,1)} %get-tuple-element.15.acts_hbm, ...), custom_call_target="tpu_custom_call" | custom-call | tf_op jit(solution)/shard_map/weight_grads/pallas_call | solution.py:669

commit v3 on v2

--- a/solution.py
+++ b/solution.py
@@ -12,6 +12,7 @@
 UNIT = 4608
 BLOCK = 128
 MESH = pl.DeviceIdType.MESH
+SHARED = 384
 TOP = 80
 
 
@@ -52,7 +53,6 @@
     levels,
     gate_f,
     up_f,
-    back_f,
     acts,
     part,
     part_sib,
@@ -75,6 +75,7 @@
     rs_sem,
     act_sem,
     own_sem,
+    share_sem,
 ):
     feats, toks = tokens_in.shape
     rows = 2 * feats
@@ -260,58 +261,71 @@
         await_(levels.at[2], lev_sem.at[1])
         rput(levels.at[1], levels.at[3], misc_send.at[2], lev_sem.at[2], y_p)
 
+    local = gate_w.shape[1]
+    kept = (local, local - SHARED, local - SHARED, local)
+
     def gate_step(s):
-        gate_f[...] = contract(xx[0, s], gate_w[...], 0, 0)
+        gate_f[:, : kept[s]] = contract(xx[0, s], gate_w[:, : kept[s]], 0, 0)
 
     def up_step(s):
-        up_f[...] = contract(xx[0, s], up_w[...], 0, 0)
-
-    def back_step(s):
-        back_f[...] = contract(xx[1, s], down_w[...], 0, 1)
+        up_f[:, : kept[s]] = contract(xx[0, s], up_w[:, : kept[s]], 0, 0)
 
     def act_copy(s):
         return pltpu.make_async_copy(
-            acts.at[s % 2], acts_hbm.at[:, pl.ds(s * toks, toks), :], act_sem.at[s]
+            acts.at[s % 2, :, :, pl.ds(0, kept[s])],
+            acts_hbm.at[:, pl.ds(s * toks, toks), pl.ds(0, kept[s])],
+            act_sem.at[s],
         )
 
-    def point_step(s, b):
-        local = gate_w.shape[1]
-        if s == 3 and b == 0:
+    def shared(slot):
+        return acts_hbm.at[:, pl.ds(slot * toks, toks), pl.ds(local - SHARED, SHARED)]
+
+    def share_acts():
+        act_copy(0).wait()
+        rput(shared(0), shared(1), misc_send.at[10], share_sem.at[0], y_p)
+        rput(shared(0), shared(2), misc_send.at[11], share_sem.at[1], y_m)
+
+    def await_shared():
+        await_(shared(1), share_sem.at[0])
+        await_(shared(2), share_sem.at[1])
+
+    def back_step(s):
+        n = kept[s]
+        if s == 3:
             await_(levels.at[3], lev_sem.at[2])
-        if s >= 2 and b == 0:
-            act_copy(s - 2).wait()
+            act_copy(1).wait()
         width = jnp.left_shift(jnp.full(levels.shape[1:], UNIT, jnp.int32), levels[s])
         mask = jnp.where(c * local < width, 1.0, 0.0).astype(F32)
-        keep = jnp.broadcast_to(mask[b : b + 1, 0:1], (16, local))
-
-        @pl.loop(0, BLOCK // 16)
-        def _(k):
-            r = pl.ds(pl.multiple_of(b * BLOCK + k * 16, 16), 16)
-            act, slope = gelu_pair(gate_f[r, :])
-            up = up_f[r, :] * keep
-            back = back_f[r, :] * keep
-            acts[s % 2, 2, r, :] = (act * up).astype(BF)
-            acts[s % 2, 0, r, :] = (back * up * slope).astype(BF)
-            acts[s % 2, 1, r, :] = (back * act).astype(BF)
-
-        if b == toks // BLOCK - 1:
-            act_copy(s).start()
+        back_all = contract(xx[1, s], down_w[:n, :], 0, 1)
+        for b in range(toks // BLOCK):
+            keep = jnp.broadcast_to(mask[b : b + 1, 0:1], (16, n))
+            for k in range(BLOCK // 16):
+                start = b * BLOCK + k * 16
+                r = pl.ds(start, 16)
+                act, slope = gelu_pair(gate_f[r, :n])
+                up = up_f[r, :n] * keep
+                back = back_all[start : start + 16] * keep
+                acts[s % 2, 2, r, :n] = (act * up).astype(BF)
+                acts[s % 2, 0, r, :n] = (back * up * slope).astype(BF)
+                acts[s % 2, 1, r, :n] = (back * act).astype(BF)
+        act_copy(s).start()
 
     third = xx.shape[2] // 3
 
     def out_step(t):
         part[0, pl.ds(t * third, third), :] = contract(
-            down_w[:, pl.ds(t * third, third)], acts[0, 2], 0, 1
-        ).astype(BF)
+            acts[0, 2], down_w[:, pl.ds(t * third, third)], 1, 0
+        ).T.astype(BF)
 
     def toward_step(t):
         r = pl.ds(t * third, third)
         part[1, r, :] = (
-            contract(gate_w[r, :], acts[0, 0], 1, 1) + contract(up_w[r, :], acts[0, 1], 1, 1)
-        ).astype(BF)
-
-    def rs_0():
-        rput(part.at[o], part_sib, misc_send.at[3], rs_sem.at[0], sib)
+            contract(acts[0, 0], gate_w[r, :], 1, 1) + contract(acts[0, 1], up_w[r, :], 1, 1)
+        ).T.astype(BF)
+
+    def rs_0(t):
+        r = pl.ds(t * third, third)
+        rput(part.at[o, r, :], part_sib.at[r, :], misc_send.at[3], rs_sem.at[(0, 18, 19)[t]], sib)
 
     def add_into(start, n, other):
         r = pl.ds(pl.multiple_of(start, 16), n)
@@ -321,7 +335,8 @@
         return part.at[h, pl.ds(row(d1, d2) + lo, rows if n is None else n), :]
 
     def rs_1():
-        await_(part_sib, rs_sem.at[0])
+        for t in range(3):
+            await_(part_sib.at[pl.ds(t * third, third), :], rs_sem.at[(0, 18, 19)[t]])
 
         @pl.loop(0, 16)
         def _(k):
@@ -389,115 +404,107 @@
 
     ev_a(0)
     y_send()
-    ev_m(0, 0)
     ev_b2(0)
     ev_b1(0)
     ev_c(0)
-    ev_p(0, 0)
-    ev_p(0, 2)
-    ev_e(0, 0)
+    ev_m(0, 0)
+    ev_m(0, 2)
     ev_p(0, 1)
-    ev_m(0, 2)
+    ev_m(0, 1)
     ev_p(0, 3)
     ev_a(1)
-    ev_m(0, 1)
+    ev_p(0, 0)
     ev_a(2)
     y_forward()
+    ev_p(0, 2)
     loads[0].wait()
     loads[1].wait()
     chunk_step(0)
+    ev_e(0, 0)
     ev_m(0, 3)
     chunk_step(1)
     ev_e(0, 2)
     ev_e(0, 3)
-    ev_b2(1)
+    ev_b1(1)
     ev_e(0, 1)
     chunk_step(2)
     chunk_step(3)
     ev_a(3)
-    ev_b1(1)
     ev_f(0)
+    ev_m(1, 0)
+    ev_b2(1)
+    ev_b1(2)
+    ev_p(1, 0)
+    ev_b2(2)
     loads[2].wait()
     back_step(0)
+    ev_p(2, 3)
+    ev_e(1, 0)
+    out_step(0)
+    out_step(1)
+    share_acts()
+    ev_b2(3)
+    ev_m(1, 3)
+    out_step(2)
+    ev_m(1, 1)
+    toward_step(0)
+    rs_0(0)
+    ev_b1(3)
+    ev_p(1, 3)
+    ev_p(1, 1)
+    ev_c(1)
+    toward_step(1)
+    rs_0(1)
+    ev_m(1, 2)
+    ev_p(1, 2)
     ev_e(2, 0)
-    point_step(0, 0)
-    ev_p(2, 3)
-    point_step(0, 1)
-    point_step(0, 2)
-    out_step(0)
-    ev_m(1, 3)
-    ev_p(1, 0)
-    out_step(1)
-    out_step(2)
-    ev_b1(2)
-    ev_b2(3)
-    ev_b2(2)
-    ev_p(1, 3)
-    toward_step(0)
+    ev_e(2, 2)
+    ev_e(1, 2)
+    toward_step(2)
+    rs_0(2)
+    ev_e(1, 1)
+    ev_c(3)
+    ev_e(1, 3)
+    ev_p(2, 0)
+    ev_e(2, 3)
     ev_m(2, 3)
-    ev_c(1)
-    ev_e(1, 0)
-    ev_b1(3)
-    ev_m(2, 0)
-    ev_p(1, 2)
-    ev_e(2, 2)
-    toward_step(1)
-    ev_p(1, 1)
-    ev_e(1, 2)
-    ev_e(1, 3)
-    ev_m(1, 2)
-    ev_m(1, 0)
-    ev_m(1, 1)
-    toward_step(2)
-    ev_e(1, 1)
-    rs_0()
     ev_f(1)
-    ev_c(3)
     gate_step(1)
     rs_1()
+    ev_p(3, 1)
+    ev_p(3, 0)
+    ev_e(2, 1)
+    ev_m(3, 2)
     ev_c(2)
-    ev_p(3, 1)
-    up_step(1)
-    ev_e(2, 1)
-    ev_p(2, 0)
+    ev_m(2, 0)
     ev_p(2, 2)
     ev_m(2, 2)
     ev_m(2, 1)
+    up_step(1)
     ev_m(3, 0)
-    ev_m(3, 2)
+    ev_p(3, 2)
+    ev_m(3, 3)
+    ev_p(3, 3)
     ev_p(2, 1)
-    ev_p(3, 3)
     back_step(1)
-    ev_e(2, 3)
-    ev_m(3, 1)
-    point_step(1, 0)
-    point_step(1, 1)
     rs_2()
-    ev_m(3, 3)
-    point_step(1, 2)
     ev_f(2)
     gate_step(2)
     up_step(2)
     ev_e(3, 0)
+    ev_e(3, 2)
     ev_e(3, 3)
+    ev_e(3, 1)
+    ev_m(3, 1)
     back_step(2)
-    ev_e(3, 2)
-    ev_e(3, 1)
-    ev_p(3, 2)
-    ev_p(3, 0)
-    point_step(2, 0)
-    point_step(2, 1)
     rs_3()
-    point_step(2, 2)
     ev_f(3)
     gate_step(3)
     rs_4()
     up_step(3)
+    rs_5()
     back_step(3)
-    rs_5()
-    point_step(3, 0)
-    point_step(3, 1)
-    point_step(3, 2)
+    await_shared()
     rs_6()
     act_copy(2).wait()
     act_copy(3).wait()
@@ -521,6 +528,8 @@
     await_(block_one, misc_send.at[7])
     await_(fin_sib, misc_send.at[8])
     await_(xx.at[0, 0, pl.ds(0, 12 * rows), :], misc_send.at[9])
+    await_(shared(0), misc_send.at[10])
+    await_(shared(0), misc_send.at[11])
 
 
 def layer(tokens, cotangent, prefix, gate_weight, up_weight, down_weight):
@@ -549,7 +558,6 @@
             pltpu.VMEM((4, 8, 128), jnp.int32),
             pltpu.VMEM((toks, local), F32),
             pltpu.VMEM((toks, local), F32),
-            pltpu.VMEM((toks, local), F32),
             pltpu.VMEM((2, 3, toks, local), BF),
             pltpu.VMEM((2, width, toks), BF),
             pltpu.VMEM((width, toks), BF),
@@ -568,10 +576,11 @@
             dma((4, 4)),
             dma((4,)),
             dma((4,)),
-            dma((10,)),
-            dma((18,)),
+            dma((12,)),
+            dma((20,)),
             dma((4,)),
             dma((2, 4)),
+            dma((2,)),
         ],
         compiler_params=pltpu.CompilerParams(
             collective_id=0, has_side_effects=True, vmem_limit_bytes=67043328
@@ -611,11 +620,9 @@
             acts_hbm.at[k, halves[j]], acts.at[k, halves[j]], in_sem.at[4 + 2 * k + j]
         )
 
-    for k in range(3):
-        for j in range(2):
-            if k != 1:
-                own_load(k // 2, j).start()
-            acts_load(k, j).start()
+    for j in range(2):
+        own_load(0, j).start()
+        acts_load(0, j).start()
     brought = [
         pltpu.make_async_copy(src, small.at[j], small_sem.at[j])
         for j, src in enumerate((first_hbm, second_hbm))
@@ -640,6 +647,18 @@
                 own_load(a, j).wait()
 
             acts_load(k, j).wait()
+            if j == 0:
+
+                @pl.when(k == 1)
+                def _():
+                    own_load(1, 0).start()
+                    own_load(1, 1).start()
+
+                @pl.when(k < 2)
+                def _():
+                    acts_load(k + 1, 0).start()
+                    acts_load(k + 1, 1).start()
+
             term = jnp.dot(
                 own[a, :, halves[j]], acts[k, halves[j], :], preferred_element_type=F32
             )

time: 94.3 us -> 92.6 us (0.982); the launches traced: 92.5 us -> 92.4 us
  no operation moved by 1% of the time
where the time goes in v3:
time: 92.6 us; the launch traced here: 92.4 us
  Pallas kernels  91.6 us (99%)
    pallas_call x1, Pallas kernels, layer(): pl.pallas_call(layer_kernel, out_shape=(jax.ShapeDtypeStruct((3, 4 * toks...  79.8 us
    pallas_call x1, Pallas kernels, weight_grads(): pl.pallas_call(grads_kernel, out_shape=(grad, grad, grad, like, like), in...  11.7 us

profile of v3, /device:TPU:0, one launch (start us, length us, event | category | flops | bytes accessed | tf_op | source)
XLA Modules:
  0.0 92.4 jit_solution(14912687339014563085)
XLA Ops:
  0.6 79.8 %layer.1 = (bf16[3,1536,1152]{2,1,0:T(8,128)(2,1)}, bf16[2,576,1536]{2,1,0:T(8,128)(2,1)}, bf16[72,384]{1,0:T(8,128)(2,1)}, bf16[72,384]{1,0:T(8,128)(2,1)}) custom-call(bf16[72,384]{1,0:T(8,128)(2,1)} %bitcast.5, bf16[72,384]{1,0:T(8,128)(2,1)} %bitcast.6, s32[3]{0:T(128)} %prefix_in.1, bf16[2304,1152]{1,0:T(8,128)(2,1)} %gate_hbm.1, ...), custom_call_target="tpu_custom_call" | custom-call | tf_op jit(solution)/shard_map/layer/pallas_call | solution.py:542
  80.5 11.7 %weight_grads.1 = (bf16[576,1152]{1,0:T(8,128)(2,1)}, bf16[576,1152]{1,0:T(8,128)(2,1)}, bf16[576,1152]{1,0:T(8,128)(2,1)}, bf16[72,384]{1,0:T(8,128)(2,1)}, bf16[72,384]{1,0:T(8,128)(2,1)}) custom-call(bf16[2,576,1536]{2,1,0:T(8,128)(2,1)} %get-tuple-element.14.own_hbm, bf16[3,1536,1152]{2,1,0:T(8,128)(2,1)} %get-tuple-element.15.acts_hbm, ...), custom_call_target="tpu_custom_call" | custom-call | tf_op jit(solution)/shard_map/weight_grads/pallas_call | solution.py:688

commit v4 on v3

--- a/solution.py
+++ b/solution.py
@@ -403,109 +403,109 @@
         grad_ref[...] = jnp.where(h == 0, other, mine).astype(BF)
 
     ev_a(0)
+    ev_m(0, 0)
+    ev_b2(0)
     y_send()
-    ev_b2(0)
     ev_b1(0)
     ev_c(0)
-    ev_m(0, 0)
+    ev_p(0, 0)
+    ev_e(0, 0)
+    ev_p(0, 1)
     ev_m(0, 2)
-    ev_p(0, 1)
+    ev_p(0, 3)
     ev_m(0, 1)
-    ev_p(0, 3)
     ev_a(1)
-    ev_p(0, 0)
     ev_a(2)
     y_forward()
-    ev_p(0, 2)
     loads[0].wait()
     loads[1].wait()
     chunk_step(0)
-    ev_e(0, 0)
     ev_m(0, 3)
+    ev_e(0, 1)
+    ev_p(0, 2)
     chunk_step(1)
     ev_e(0, 2)
     ev_e(0, 3)
+    chunk_step(2)
     ev_b1(1)
-    ev_e(0, 1)
-    chunk_step(2)
+    ev_e(2, 0)
+    ev_b2(1)
     chunk_step(3)
+    ev_f(0)
     ev_a(3)
-    ev_f(0)
-    ev_m(1, 0)
-    ev_b2(1)
-    ev_b1(2)
-    ev_p(1, 0)
-    ev_b2(2)
     loads[2].wait()
     back_step(0)
-    ev_p(2, 3)
-    ev_e(1, 0)
+    ev_p(1, 3)
     out_step(0)
+    ev_b1(2)
+    ev_b2(2)
+    ev_m(1, 3)
     out_step(1)
+    ev_m(1, 0)
     share_acts()
+    ev_p(1, 0)
+    out_step(2)
+    ev_p(1, 1)
     ev_b2(3)
-    ev_m(1, 3)
-    out_step(2)
+    toward_step(0)
+    ev_m(2, 0)
+    ev_m(1, 2)
+    ev_b1(3)
+    ev_p(3, 0)
+    ev_m(2, 3)
+    ev_p(2, 0)
+    ev_c(2)
+    ev_e(1, 2)
     ev_m(1, 1)
-    toward_step(0)
+    ev_p(1, 2)
     rs_0(0)
-    ev_b1(3)
-    ev_p(1, 3)
-    ev_p(1, 1)
+    ev_e(1, 1)
     ev_c(1)
     toward_step(1)
+    ev_e(1, 0)
+    ev_e(1, 3)
+    ev_m(2, 1)
+    ev_e(2, 1)
+    ev_e(2, 2)
     rs_0(1)
-    ev_m(1, 2)
-    ev_p(1, 2)
-    ev_e(2, 0)
-    ev_e(2, 2)
-    ev_e(1, 2)
     toward_step(2)
+    ev_f(1)
     rs_0(2)
-    ev_e(1, 1)
+    ev_m(3, 0)
     ev_c(3)
-    ev_e(1, 3)
-    ev_p(2, 0)
+    gate_step(1)
+    ev_p(2, 2)
+    rs_1()
+    ev_p(2, 1)
+    ev_p(2, 3)
+    ev_m(2, 2)
+    ev_p(3, 2)
     ev_e(2, 3)
-    ev_m(2, 3)
-    ev_f(1)
-    gate_step(1)
-    rs_1()
+    up_step(1)
+    ev_e(3, 0)
     ev_p(3, 1)
-    ev_p(3, 0)
-    ev_e(2, 1)
+    ev_f(2)
+    ev_p(3, 3)
     ev_m(3, 2)
-    ev_c(2)
-    ev_m(2, 0)
-    ev_p(2, 2)
-    ev_m(2, 2)
-    ev_m(2, 1)
-    up_step(1)
-    ev_m(3, 0)
-    ev_p(3, 2)
+    back_step(1)
+    gate_step(2)
+    rs_2()
+    ev_e(3, 1)
+    up_step(2)
     ev_m(3, 3)
-    ev_p(3, 3)
-    ev_p(2, 1)
-    back_step(1)
-    rs_2()
-    ev_f(2)
-    gate_step(2)
-    up_step(2)
-    ev_e(3, 0)
+    ev_m(3, 1)
     ev_e(3, 2)
     ev_e(3, 3)
-    ev_e(3, 1)
-    ev_m(3, 1)
     back_step(2)
-    rs_3()
     ev_f(3)
     gate_step(3)
+    rs_3()
+    up_step(3)
     rs_4()
-    up_step(3)
+    back_step(3)
     rs_5()
-    back_step(3)
+    rs_6()
     await_shared()
-    rs_6()
     act_copy(2).wait()
     act_copy(3).wait()
     for s in range(4):
@@ -620,9 +620,11 @@
             acts_hbm.at[k, halves[j]], acts.at[k, halves[j]], in_sem.at[4 + 2 * k + j]
         )
 
-    for j in range(2):
-        own_load(0, j).start()
-        acts_load(0, j).start()
+    for k in range(3):
+        for j in range(2):
+            if k != 1:
+                own_load(k // 2, j).start()
+            acts_load(k, j).start()
     brought = [
         pltpu.make_async_copy(src, small.at[j], small_sem.at[j])
         for j, src in enumerate((first_hbm, second_hbm))
@@ -647,18 +649,6 @@
                 own_load(a, j).wait()
 
             acts_load(k, j).wait()
-            if j == 0:
-
-                @pl.when(k == 1)
-                def _():
-                    own_load(1, 0).start()
-                    own_load(1, 1).start()
-
-                @pl.when(k < 2)
-                def _():
-                    acts_load(k + 1, 0).start()
-                    acts_load(k + 1, 1).start()
-
             term = jnp.dot(
                 own[a, :, halves[j]], acts[k, halves[j], :], preferred_element_type=F32
             )

time: 92.6 us -> 87.7 us (0.947); the launches traced: 92.4 us -> 86.3 us
  Pallas kernels: 91.6 us -> 85.5 us
    pallas_call x1, Pallas kernels: 79.8 us -> 73.9 us  [layer(): pl.pallas_call(layer_kernel, out_shape=(jax.ShapeDtypeStruct((3, 4 * toks...]
where the time goes in v4:
time: 87.7 us; the launch traced here: 86.3 us
  Pallas kernels  85.5 us (97%)
    pallas_call x1, Pallas kernels, layer(): pl.pallas_call(layer_kernel, out_shape=(jax.ShapeDtypeStruct((3, 4 * toks...  73.9 us
    pallas_call x1, Pallas kernels, weight_grads(): pl.pallas_call(grads_kernel, out_shape=(grad, grad, grad, like, like), in...  11.5 us

profile of v4, /device:TPU:0, one launch (start us, length us, event | category | flops | bytes accessed | tf_op | source)
XLA Modules:
  0.0 86.3 jit_solution(656650884339372882)
XLA Ops:
  0.6 73.9 %layer.1 = (bf16[3,1536,1152]{2,1,0:T(8,128)(2,1)}, bf16[2,576,1536]{2,1,0:T(8,128)(2,1)}, bf16[72,384]{1,0:T(8,128)(2,1)}, bf16[72,384]{1,0:T(8,128)(2,1)}) custom-call(bf16[72,384]{1,0:T(8,128)(2,1)} %bitcast.5, bf16[72,384]{1,0:T(8,128)(2,1)} %bitcast.6, s32[3]{0:T(128)} %prefix_in.1, bf16[2304,1152]{1,0:T(8,128)(2,1)} %gate_hbm.1, ...), custom_call_target="tpu_custom_call" | custom-call | tf_op jit(solution)/shard_map/layer/pallas_call | solution.py:542
  74.6 11.5 %weight_grads.1 = (bf16[576,1152]{1,0:T(8,128)(2,1)}, bf16[576,1152]{1,0:T(8,128)(2,1)}, bf16[576,1152]{1,0:T(8,128)(2,1)}, bf16[72,384]{1,0:T(8,128)(2,1)}, bf16[72,384]{1,0:T(8,128)(2,1)}) custom-call(bf16[2,576,1536]{2,1,0:T(8,128)(2,1)} %get-tuple-element.14.own_hbm, bf16[3,1536,1152]{2,1,0:T(8,128)(2,1)} %get-tuple-element.15.acts_hbm, ...), custom_call_target="tpu_custom_call" | custom-call | tf_op jit(solution)/shard_map/weight_grads/pallas_call | solution.py:678
